TPU v7x, 8 devices: a whole 2x2x1 slice. The times are simulated.
8 devices in a mesh: dp: 1 (over z), ep: 8 (over y, x, core).
Axes of the slice: x: 2, y: 2, z: 1, core: 2. Of those that a mesh axis runs over, the one named last changes fastest.
Arguments:
- hidden: bfloat16 [8, 128, 2048], P(('dp', 'ep'))
- expert_ids: int32 [8, 128, 8], P(('dp', 'ep'))
- slot_ids: int32 [8, 128, 8], P(('dp', 'ep'))
- attn_norm: bfloat16 [2048], replicated
- w_query: bfloat16 [2048, 2048], replicated
- w_key: bfloat16 [2048, 2048], replicated
- w_value: bfloat16 [2048, 2048], replicated
- w_out: bfloat16 [16, 128, 2048], replicated
- ffn_norm: bfloat16 [2048], replicated
- ffn_gate: bfloat16 [2048, 8192], replicated
- ffn_up: bfloat16 [2048, 8192], replicated
- ffn_down: bfloat16 [8192, 2048], replicated
- moe_norm: bfloat16 [2048], replicated
- w_router: bfloat16 [2048, 64], replicated
- exp_gate: bfloat16 [64, 2048, 1024], P('ep')
- exp_up: bfloat16 [64, 2048, 1024], P('ep')
- exp_down: bfloat16 [64, 1024, 2048], P('ep')
Outputs:
- output: bfloat16 [8, 128, 2048], P(('dp', 'ep'))
All inputs are finite; a program needn't handle non-finite values.
Results may differ from a plain program's by a relative error of at most 0.00942246.
Values are sent between devices in bfloat16 or wider.
A program may use at most 1 GiB of HBM per device.

v0:
```python
import jax
import jax.numpy as jnp
from jax import lax
from jax.sharding import PartitionSpec as P, NamedSharding

RMS_EPS = 1e-6
ROPE_BASE = 10000.0
CAP_FACTOR = 3


def rms_norm(row_vals, norm_scale):
    as_float = row_vals.astype(jnp.float32)
    inv_rms = lax.rsqrt(jnp.mean(as_float * as_float, axis=-1, keepdims=True) + RMS_EPS)
    return (as_float * inv_rms * norm_scale.astype(jnp.float32)).astype(jnp.bfloat16)


def rotary(head_vals):
    seq_len, head_dim = head_vals.shape[1], head_vals.shape[3]
    half_dim = head_dim // 2
    inv_freq = ROPE_BASE ** (-2.0 * jnp.arange(half_dim, dtype=jnp.float32) / head_dim)
    angles = jnp.arange(seq_len, dtype=jnp.float32)[:, None] * inv_freq[None, :]
    cos_t = jnp.cos(angles)[:, None, :]
    sin_t = jnp.sin(angles)[:, None, :]
    first_half = head_vals[..., :half_dim]
    second_half = head_vals[..., half_dim:]
    return jnp.concatenate([first_half * cos_t - second_half * sin_t, second_half * cos_t + first_half * sin_t], axis=-1)


def dense_branch(hidden, attn_norm, w_query, w_key, w_value, w_out, ffn_norm, ffn_gate, ffn_up, ffn_down):
    n_seqs, seq_len, model_dim = hidden.shape
    n_heads, head_dim = w_out.shape[0], w_out.shape[1]
    kv_heads = w_key.shape[1] // head_dim
    q_per_kv = n_heads // kv_heads
    normed = rms_norm(hidden, attn_norm)
    queries = rotary(jnp.einsum('bsd,de->bse', normed, w_query, preferred_element_type=jnp.float32).reshape(n_seqs, seq_len, n_heads, head_dim))
    queries = queries.astype(jnp.bfloat16).reshape(n_seqs, seq_len, kv_heads, q_per_kv, head_dim)
    key_vals = rotary(jnp.einsum('bsd,de->bse', normed, w_key, preferred_element_type=jnp.float32).reshape(n_seqs, seq_len, kv_heads, head_dim)).astype(jnp.bfloat16)
    values = jnp.einsum('bsd,de->bse', normed, w_value, preferred_element_type=jnp.float32).astype(jnp.bfloat16).reshape(n_seqs, seq_len, kv_heads, head_dim)
    scores = jnp.einsum('bsgrd,btgd->bgrst', queries, key_vals, preferred_element_type=jnp.float32) * head_dim ** -0.5
    causal = jnp.arange(seq_len)[:, None] >= jnp.arange(seq_len)[None, :]
    attn_prob = jax.nn.softmax(jnp.where(causal, scores, -jnp.inf), axis=-1).astype(jnp.bfloat16)
    context = jnp.einsum('bgrst,btgd->bsgrd', attn_prob, values, preferred_element_type=jnp.float32).astype(jnp.bfloat16)
    context = context.reshape(n_seqs, seq_len, n_heads, head_dim)
    attn_out = (hidden.astype(jnp.float32) + jnp.einsum('bshd,hde->bse', context, w_out, preferred_element_type=jnp.float32)).astype(jnp.bfloat16)
    normed_ffn = rms_norm(attn_out, ffn_norm)
    hidden_act = (jax.nn.silu(jnp.einsum('bsd,df->bsf', normed_ffn, ffn_gate, preferred_element_type=jnp.float32)) * jnp.einsum('bsd,df->bsf', normed_ffn, ffn_up, preferred_element_type=jnp.float32)).astype(jnp.bfloat16)
    return attn_out.astype(jnp.float32) + jnp.einsum('bsf,fd->bsd', hidden_act, ffn_down, preferred_element_type=jnp.float32)


def route_gates(normed, w_router, choice_ids):
    logits = jnp.einsum('...d,de->...e', normed, w_router, preferred_element_type=jnp.float32)
    return jax.nn.softmax(jnp.take_along_axis(logits, choice_ids, axis=-1), axis=-1)


def expert_ffn(expert_in, exp_gate, exp_up, exp_down):
    z_gate = jnp.einsum('egcd,edf->egcf', expert_in, exp_gate, preferred_element_type=jnp.float32)
    z_up = jnp.einsum('egcd,edf->egcf', expert_in, exp_up, preferred_element_type=jnp.float32)
    hidden_act = (jax.nn.silu(z_gate) * z_up).astype(jnp.bfloat16)
    return jnp.einsum('egcf,efd->egcd', hidden_act, exp_down, preferred_element_type=jnp.float32).astype(jnp.bfloat16)


def solution(mesh):
    group_size = mesh.shape['ep']
    row_spec = P(('dp', 'ep'), None, None)
    vec_spec = P(None)
    mat_spec = P(None, None)
    cube_spec = P(None, None, None)
    expert_spec = P('ep', None, None)

    def per_device(hidden, expert_ids, slot_ids, attn_norm, w_query, w_key, w_value, w_out, ffn_norm, ffn_gate, ffn_up, ffn_down, moe_norm, w_router, exp_gate, exp_up, exp_down):
        n_seqs, seq_len, model_dim = hidden.shape
        top_k = expert_ids.shape[-1]
        tokens = n_seqs * seq_len
        local_experts = exp_gate.shape[0]
        n_experts = local_experts * group_size
        capacity = CAP_FACTOR * tokens * top_k // n_experts
        normed = rms_norm(hidden.reshape(tokens, model_dim), moe_norm)
        choice_ids = expert_ids.reshape(tokens, top_k)
        gate_vals = route_gates(normed, w_router, choice_ids)
        buf_pos = choice_ids * capacity + slot_ids.reshape(tokens, top_k)
        owner_tok = jnp.full((n_experts * capacity,), tokens, jnp.int32).at[buf_pos.reshape(-1)].set(jnp.arange(tokens * top_k, dtype=jnp.int32) // top_k)
        padded = jnp.concatenate([normed, jnp.zeros((1, model_dim), jnp.bfloat16)], axis=0)
        send_buf = jnp.take(padded, owner_tok, axis=0).reshape(group_size, local_experts, capacity, model_dim)
        recv_buf = lax.all_to_all(send_buf, 'ep', 0, 1)
        expert_out = expert_ffn(recv_buf, exp_gate, exp_up, exp_down)
        back_buf = lax.all_to_all(expert_out, 'ep', 1, 0).reshape(n_experts * capacity, model_dim)
        picked = jnp.take(back_buf, buf_pos.reshape(-1), axis=0).reshape(tokens, top_k, model_dim)
        moe_out = jnp.sum(gate_vals[:, :, None] * picked.astype(jnp.float32), axis=1)
        dense_out = dense_branch(hidden, attn_norm, w_query, w_key, w_value, w_out, ffn_norm, ffn_gate, ffn_up, ffn_down).reshape(tokens, model_dim)
        return (dense_out + moe_out).astype(jnp.bfloat16).reshape(n_seqs, seq_len, model_dim)

    return jax.shard_map(per_device, mesh=mesh, in_specs=(row_spec, row_spec, row_spec, vec_spec, mat_spec, mat_spec, mat_spec, cube_spec, vec_spec, mat_spec, mat_spec, mat_spec, vec_spec, mat_spec, expert_spec, expert_spec, expert_spec), out_specs=row_spec, check_vma=False)
```

profile of v0, /device:TPU:0, one launch (start us, length us, event | category | flops | bytes accessed | tf_op | source)
XLA Modules:
  0.0 454.1 jit_solution(15405062634907459957)
XLA Ops:
  0.0 0.7 multiply_add_fusion
  0.8 0.1 copy.51
  0.9 0.1 add.144
  1.0 4.3 scatter_custom_fusion
  5.3 1.2 fusion.32
  6.6 0.7 convert_element_type.92
  7.3 0.1 broadcast_in_dim.66
  7.4 0.0 copy-done.5
  7.4 1.2 fusion.34
  8.7 16.0 %gather_fusion = bf16[3072,2048]{1,0:T(8,128)(2,1)} fusion(bf16[129,2048]{1,0:T(8,128)(2,1)S(1)} %concatenate.32, s32[3072]{0:T(1024)S(1)} %fusion.71), kind=kCustom, calls=%fused_computation | custom fusion | bytes 25178112 | tf_op jit(solution)/shard_map/jit(_take)/gather | solution.py:83
  24.7 6.5 %select_bitcast_fusion = bf16[8,8,1,48,2048]{4,3,1,2,0:T(8,128)(2,1)S(1)} fusion(bf16[8,8,1,48,2048]{4,3,1,0,2:T(8,128)(2,1)} %bitcast.169, pred[8,8,48]{2,1,0:T(8,128)(4,1)S(1)} %broadcast_in_dim.66), kind=kLoop, calls=%fused_computation.14 | loop fusion | flops 6291456 | bytes 25168896 | tf_op jit(solution)/shard_map/jit(_take)/select_n | solution.py:83
  31.2 143.2 %all_to_all.30 = bf16[8,8,1,48,2048]{4,3,1,2,0:T(8,128)(2,1)} all-to-all(bf16[8,8,1,48,2048]{4,3,1,2,0:T(8,128)(2,1)S(1)} %select_bitcast_fusion), channel_id=1, replica_groups=mesh['dp'=1,'ep'=8] {'ep'}, dimensions={0} | all-to-all | bytes 25165824 | tf_op jit(solution)/shard_map/all_to_all | solution.py:84
  174.4 27.4 %fusion.2 = f32[8,8,48,1024]{3,2,1,0:T(8,128)} fusion(bf16[8,2048,1024]{2,1,0:T(8,128)(2,1)} %param.32, bf16[8,8,1,48,2048]{4,3,1,2,0:T(8,128)(2,1)} %all_to_all.30), kind=kOutput, calls=%fused_computation.6 | convolution fusion | flops 12884901888 | bytes 58720256 | tf_op jit(solution)/shard_map/egcd,edf->egcf/dot_general | solution.py:57
  201.8 28.6 %multiply_convert_fusion = bf16[8,8,48,1024]{3,2,1,0:T(8,128)(2,1)} fusion(f32[8,8,48,1024]{3,2,1,0:T(8,128)} %fusion.2, bf16[8,2048,1024]{2,1,0:T(8,128)(2,1)} %param.31, bf16[8,8,1,48,2048]{4,3,1,2,0:T(8,128)(2,1)} %all_to_all.30), kind=kOutput, calls=%fused_computation.13 | convolution fusion | flops 12903776256 | bytes 65011712 | tf_op jit(solution)/shard_map/egcd,edf->egcf/dot_general | solution.py:56
  230.4 22.1 %convert_bitcast_fusion = bf16[1,8,8,48,2048]{4,3,2,1,0:T(8,128)(2,1)} fusion(bf16[8,8,48,1024]{3,2,1,0:T(8,128)(2,1)} %multiply_convert_fusion, bf16[8,1024,2048]{2,1,0:T(8,128)(2,1)} %param.33), kind=kOutput, calls=%fused_computation.12 | convolution fusion | flops 12891193344 | bytes 52428800 | tf_op jit(solution)/shard_map/egcf,efd->egcd/dot_general | solution.py:59
  252.5 10.8 %copy.54 = bf16[1,8,8,48,2048]{4,3,1,0,2:T(8,128)(2,1)} copy(bf16[1,8,8,48,2048]{4,3,2,1,0:T(8,128)(2,1)} %convert_bitcast_fusion) | data formatting | bytes 25165824 | tf_op jit(solution)/shard_map/broadcast_in_dim | solution.py:86
  263.3 4.4 all-to-all-start.1
  267.8 0.1 copy.48
  267.9 0.7 copy.50
  268.6 0.1 copy.49
  268.7 0.1 reshape.389
  268.8 0.3 fusion.89
  269.1 0.0 copy-start.1
  269.1 7.0 %gather_fusion.2 = f32[1024]{0:T(1024)S(1)} fusion(f32[128,64]{0,1:T(8,128)S(1)} %fusion.89, s32[1024]{0:T(1024)S(1)} %reshape.389), kind=kCustom, calls=%fused_computation.2 | custom fusion | bytes 16384 | tf_op jit(solution)/shard_map/jit(take_along_axis)/gather | solution.py:52
  276.2 0.1 reshape.392
  276.3 0.0 copy-start.2
  276.3 0.2 fusion.35
  276.5 4.7 %convolution_convert_fusion = bf16[128,2048]{1,0:T(8,128)(2,1)S(1)} fusion(bf16[2048,2048]{1,0:T(8,128)(2,1)} %param.23, bf16[1,128,2048]{2,1,0:T(8,128)(2,1)S(1)} %copy-done.1, f32[2048]{0:T(1024)S(1)} %convert_element_type.78, f32[128]{0:T(128)S(1)} %add_rsqrt_fusion.2), kind=kOutput, calls=%fused_computation.28 | convolution fusion | flops 1075052544 | bytes 9445888 | tf_op jit(solution)/shard_map/bsd,de->bse/dot_general | solution.py:38
  281.2 0.3 copy.62
  281.5 12.3 %copy.64 = bf16[2048,2048]{1,0:T(8,128)(2,1)} copy(bf16[2048,2048]{0,1:T(8,128)(2,1)} %bitcast.170) | data formatting | bytes 16777216 | tf_op jit(solution)/shard_map/bsd,de->bse/dot_general | solution.py:35
  293.8 12.3 %copy.63 = bf16[2048,2048]{1,0:T(8,128)(2,1)} copy(bf16[2048,2048]{0,1:T(8,128)(2,1)} %bitcast.171) | data formatting | bytes 16777216 | tf_op jit(solution)/shard_map/bsd,de->bse/dot_general | solution.py:37
  306.2 0.1 fusion.82
  306.3 0.2 fusion.68
  306.5 0.2 fusion.70
  306.7 0.0 slice-start.1
  306.7 6.1 %convolution_bitcast_fusion.1 = f32[1,128,16,128]{1,3,2,0:T(8,128)S(1)} fusion(bf16[16,128,2048]{2,1,0:T(8,128)(2,1)} %bitcast.168, bf16[1,128,2048]{2,1,0:T(8,128)(2,1)S(1)} %copy-done.1, f32[2048]{0:T(1024)S(1)} %convert_element_type.78, f32[128]{0:T(128)S(1)} %add_rsqrt_fusion.2), kind=kOutput, calls=%fused_computation.38 | convolution fusion | flops 1074790400 | bytes 9970176 | tf_op jit(solution)/shard_map/bsd,de->bse/dot_general | solution.py:35
  312.8 2.5 convolution_bitcast_fusion.2
  315.3 0.3 fusion.65
  315.6 0.4 fusion.86
  316.0 0.2 fusion.38
  316.2 4.9 %multiply_reduce_fusion.1 = (f32[128]{0:T(128)S(1)}, f32[1,128,2048]{2,1,0:T(8,128)S(1)}) fusion(bf16[16,128,2048]{2,1,0:T(8,128)(2,1)} %param.24, bf16[128,16,128]{0,2,1:T(8,128)(2,1)S(1)} %bitcast.172, f32[1,16,1,128,128]{3,4,1,2,0:T(8,128)S(1)} %get-tuple-element.14, f32[16,128]{1,0:T(8,128)S(1)} %fusion.38, f32[16,128]{1,0:T(8,128)S(1)} %get-tuple-element.13, ...), kind=kOutput, calls=%fused_computation.52 | convolution fusion | flops 1143472000 | bytes 11551232 | tf_op jit(solution)/shard_map/bshd,hde->bse/dot_general | solution.py:44
  321.1 0.9 compare_and_fusion
  322.0 0.9 fusion.67
  322.9 17.1 %fusion.42 = f32[128,8192]{1,0:T(8,128)} fusion(bf16[2048,8192]{1,0:T(8,128)(2,1)} %param.26, f32[1,128,2048]{2,1,0:T(8,128)S(1)} %get-tuple-element.16, f32[2048]{0:T(1024)S(1)} %convert_element_type.87, f32[128]{0:T(128)S(1)} %add_rsqrt_fusion.1), kind=kOutput, calls=%fused_computation.57 | convolution fusion | flops 4295753728 | bytes 38806016 | tf_op jit(solution)/shard_map/bsd,df->bsf/dot_general | solution.py:46
  340.1 66.7 %all-to-all-done.1 = bf16[1,8,8,48,2048]{4,3,1,0,2:T(8,128)(2,1)} async-done(((bf16[1,8,8,48,2048]{4,3,1,0,2:T(8,128)(2,1)}), bf16[1,8,8,48,2048]{4,3,1,0,2:T(8,128)(2,1)}, u32[]{:S(2)}, u32[]{:S(2)}) %all-to-all-start.1) | async-done | bytes 12582944 | tf_op jit(solution)/shard_map/all_to_all | solution.py:86
  406.7 15.3 %gather_fusion.1 = bf16[1024,2048]{1,0:T(8,128)(2,1)} fusion(bf16[3072,2048]{1,0:T(8,128)(2,1)} %bitcast.44, s32[1024]{0:T(1024)S(1)} %broadcast_clamp_fusion), kind=kCustom, calls=%fused_computation.1 | custom fusion | bytes 8392704 | tf_op jit(solution)/shard_map/jit(_take)/gather | solution.py:87
  422.0 5.6 %multiply_reduce_fusion = f32[128,2048]{1,0:T(8,128)S(1)} fusion(bf16[1024,2048]{1,0:T(8,128)(2,1)} %gather_fusion.1, f32[128,8]{1,0:T(8,128)S(1)} %fusion.67, pred[128,8]{1,0:T(8,128)(4,1)S(1)} %compare_and_fusion), kind=kLoop, calls=%fused_computation.19 | loop fusion | flops 8126464 | bytes 5248000 | tf_op jit(solution)/shard_map/reduce_sum | solution.py:88
  427.6 26.1 %fusion.25 = bf16[1,128,2048]{2,1,0:T(8,128)(2,1)} fusion(f32[1,128,2048]{2,1,0:T(8,128)S(1)} %get-tuple-element.16, bf16[8192,2048]{1,0:T(8,128)(2,1)} %param.28, bf16[2048,8192]{1,0:T(8,128)(2,1)} %param.27, f32[128,8192]{1,0:T(8,128)} %fusion.42, f32[128,2048]{1,0:T(8,128)S(1)} %multiply_reduce_fusion, f32[2048]{0:T(1024)S(1)} %convert_element_type.87, ...), kind=kOutput, calls=%fused_computation.31 | convolution fusion | flops 8597798912 | bytes 73933312 | tf_op jit(solution)/shard_map/bsf,fd->bsd/dot_general | solution.py:47
  (33 shorter events, 0.2 us)
Async XLA Ops:
  0.0 268.8 %copy-start = (bf16[2048,64]{0,1:T(8,128)(2,1)S(1)}, bf16[2048,64]{0,1:T(8,128)(2,1)}, u32[]{:S(2)}) copy-start(bf16[2048,64]{0,1:T(8,128)(2,1)} %param.30) | copy-start | bytes 786436
  1.0 6.4 %copy-start.5 = (s32[1024,1]{0,1:T(1,128)}, s32[1024,1]{0,1:T(1,128)S(1)}, u32[]{:S(2)}) copy-start(s32[1024,1]{0,1:T(1,128)S(1)} %compare_select_fusion.3) | copy-start | bytes 12292
  263.3 4.5 copy-start.3
  263.3 4.6 %copy-start.4 = (s32[1,128,8]{1,2,0:T(8,128)S(1)}, s32[1,128,8]{1,2,0:T(8,128)}, u32[]{:S(2)}) copy-start(s32[1,128,8]{1,2,0:T(8,128)} %param.19) | copy-start | bytes 12292
  263.3 5.3 %copy-start.7 = (bf16[2048]{0:T(1024)(128)(2,1)S(1)}, bf16[2048]{0:T(1024)(128)(2,1)}, u32[]{:S(2)}) copy-start(bf16[2048]{0:T(1024)(128)(2,1)} %param.20) | copy-start | bytes 12292
  263.3 5.3 %copy-start.8 = (bf16[2048]{0:T(1024)(128)(2,1)S(1)}, bf16[2048]{0:T(1024)(128)(2,1)}, u32[]{:S(2)}) copy-start(bf16[2048]{0:T(1024)(128)(2,1)} %param.25) | copy-start | bytes 12292
  263.3 143.4 %all-to-all-start.1 = ((bf16[1,8,8,48,2048]{4,3,1,0,2:T(8,128)(2,1)}), bf16[1,8,8,48,2048]{4,3,1,0,2:T(8,128)(2,1)}, u32[]{:S(2)}, u32[]{:S(2)}) async-start(bf16[1,8,8,48,2048]{4,3,1,0,2:T(8,128)(2,1)} %copy.54), calls=%async_computation.1 | async-start | bytes 25165824 | tf_op jit(solution)/shard_map/all_to_all | solution.py:86
  269.1 7.1 %copy-start.1 = (bf16[1,128,2048]{2,1,0:T(8,128)(2,1)S(1)}, bf16[1,128,2048]{2,1,0:T(8,128)(2,1)}, u32[]{:S(2)}) copy-start(bf16[1,128,2048]{2,1,0:T(8,128)(2,1)} %param.17) | copy-start | bytes 1572868
  276.3 30.0 %copy-start.2 = (f32[128,8]{1,0:T(8,128)}, f32[128,8]{1,0:T(8,128)S(1)}, u32[]{:S(2)}) copy-start(f32[128,8]{1,0:T(8,128)S(1)} %reshape.392) | copy-start | bytes 12292
  306.1 6.7 %slice-start = ((s8[8388608]{0:T(1024)(128)(4,1)}), s8[4194304]{0:T(1024)(128)(4,1)S(1)}, s32[]{:S(2)}) async-start(s8[8388608]{0:T(1024)(128)(4,1)} %bitcast.165), calls=%async_computation.2 | async-start | bytes 8388608
  306.7 6.2 %slice-start.1 = ((s8[8388608]{0:T(1024)(128)(4,1)}), s8[4194304]{0:T(1024)(128)(4,1)S(1)}, s32[]{:S(2)}) async-start(s8[8388608]{0:T(1024)(128)(4,1)} %bitcast.165), calls=%async_computation.3 | async-start | bytes 8388608
  315.3 5.8 %copy-start.6 = (s32[1024,1]{0,1:T(1,128)S(1)}, s32[1024,1]{0,1:T(1,128)}, u32[]{:S(2)}) copy-start(s32[1024,1]{0,1:T(1,128)} %copy-done.5) | copy-start | bytes 12292
where the time goes:
time: 458 us; the launch traced here: 454 us
  blocking collectives  143 us (31%)
  matrix products  140 us (31%)
  local copies, waits for them, and re-layouts  79.8 us (17%)
  waiting for transfers between devices  66.7 us (15%)
  other arithmetic  19.1 us (4%)
    all_to_all x1, blocking collectives, per_device(): recv_buf = lax.all_to_all(send_buf, 'ep', 0, 1)  143 us
    all_to_all x1, waiting for transfers between devices, per_device(): lax.all_to_all(expert_out, 'ep', 1, 0)  66.7 us
    dot_general x1, matrix products, expert_ffn(): jnp.einsum('egcd,edf->egcf', expert_in, exp_gate, preferred_element_type=...  28.6 us
    dot_general x1, matrix products, expert_ffn(): jnp.einsum('egcd,edf->egcf', expert_in, exp_up, preferred_element_type=jn...  27.4 us
    dot_general x1, matrix products, dense_branch(): jnp.einsum('bsf,fd->bsd', hidden_act, ffn_down, preferred_element_type=jn...  26.1 us
    dot_general x1, matrix products, expert_ffn(): jnp.einsum('egcf,efd->egcd', hidden_act, exp_down, preferred_element_type...  22.1 us
    dot_general x1, matrix products, dense_branch(): jnp.einsum('bsd,df->bsf', normed_ffn, ffn_gate, preferred_element_type=jn...  17.1 us
    gather x1, local copies, waits for them, and re-layouts, per_device(): jnp.take(padded, owner_tok, axis=0)  16 us
  transfers between devices with their start and end apart: 1, of which 1 were waited for; matrix products, arithmetic and copies ran while one was open for 16% of the time, Pallas kernels for 0%

commit v1 on v0

v1 whole, which is shorter than its diff:
```python
import functools

import jax
import jax.numpy as jnp
import numpy as np
from jax import lax
from jax.experimental import pallas as pl
from jax.experimental.pallas import tpu as pltpu
from jax.sharding import PartitionSpec as P

RMS_EPS = 1e-6
ROPE_BASE = 10000.0
F32 = jnp.float32
BF16 = jnp.bfloat16

DEVS = 8
TOK = 128
DM = 2048
HEAD = 128
FF = 8192
LOCAL = 8
EFF = 1024
TOPK = 8
CAP = 48
ROWS = LOCAL * CAP
NEXP = DEVS * LOCAL
CW = 512
NCB = DM // CW
NSLOT = 8
FF_EARLY = 6

N_QKV = 12
N_OUT = 4
N_FFA = 2 * FF_EARLY
N_EGU = 4 * LOCAL
N_EDN = NCB * (LOCAL // 2)
N_FFB = 2 * (FF // CW - FF_EARLY)
N_FDN = NCB * (FF // DM)
G_QKV = 0
G_OUT = G_QKV + N_QKV
G_FFA = G_OUT + N_OUT
G_EGU = G_FFA + N_FFA
G_EDN = G_EGU + N_EGU
G_FFB = G_EDN + N_EDN
G_FDN = G_FFB + N_FFB
G_END = G_FDN + N_FDN


def aligned(index, size):
    return pl.ds(pl.multiple_of(index * size, size), size)


def dot(lhs, rhs):
    return jnp.dot(lhs, rhs, preferred_element_type=F32)


def rms(as_float, scale):
    inv_rms = lax.rsqrt(jnp.mean(as_float * as_float, axis=-1, keepdims=True) + RMS_EPS)
    return (as_float * inv_rms * scale.astype(F32)).astype(BF16)


def silu_mul(z_gate, z_up):
    return (jax.nn.silu(z_gate) * z_up).astype(BF16)


def kernel(hid, ids, slots, attn_norm, ffn_norm, moe_norm, w_router, cos_t, sin_t,
           w_query, w_key, w_value, w_out, ffn_gate, ffn_up, ffn_down, exp_gate, exp_up, exp_down,
           out,
           ring, toks, disp, hexp, pown, psib, recv0, recv1, gates, route, pay, ctx, xn, a_s, hff, facc, qs, ks, vs,
           ring_sem, ag_send, ag_recv, rt_send, rt_recv, s0_send, s0_recv, s1_send, s1_recv):
    me = lax.axis_index("ep")
    chip = me // 2
    core = me % 2
    sib = chip * 2 + 1 - core
    rel_chips = (chip + 1 - 2 * (chip % 2), (chip + 2) % 4, 3 - chip)

    def start(g, slot):
        def fetch(src, rows=None):
            dst = ring.at[slot] if rows is None else ring.at[slot, rows]
            pltpu.make_async_copy(src, dst, ring_sem.at[slot]).start()

        def within(lo, hi):
            return pl.when(jnp.logical_and(g >= lo, g < hi))

        @within(G_QKV, G_OUT)
        def _():
            col, kind = g // 3, g % 3
            for which, mat in enumerate((w_query, w_key, w_value)):
                @pl.when(kind == which)
                def _():
                    fetch(mat.at[:, aligned(col, CW)])

        @within(G_OUT, G_FFA)
        def _():
            fetch(w_out.at[:, aligned(g - G_OUT, CW)])

        def ff_pair(local, first):
            col, kind = first + local // 2, local % 2

            @pl.when(kind == 0)
            def _():
                fetch(ffn_gate.at[:, aligned(col, CW)])

            @pl.when(kind == 1)
            def _():
                fetch(ffn_up.at[:, aligned(col, CW)])

        @within(G_FFA, G_EGU)
        def _():
            ff_pair(g - G_FFA, 0)

        @within(G_EGU, G_EDN)
        def _():
            local = g - G_EGU
            expert, col, kind = local // 4, (local // 2) % 2, local % 2

            @pl.when(kind == 0)
            def _():
                fetch(exp_gate.at[expert, :, aligned(col, CW)])

            @pl.when(kind == 1)
            def _():
                fetch(exp_up.at[expert, :, aligned(col, CW)])

        @within(G_EDN, G_FFB)
        def _():
            local = g - G_EDN
            col, pair = local // 4, local % 4
            for i in range(2):
                fetch(exp_down.at[pair * 2 + i, :, aligned(col, CW)], pl.ds(i * EFF, EFF))

        @within(G_FFB, G_FDN)
        def _():
            ff_pair(g - G_FFB, FF_EARLY)

        @within(G_FDN, G_END)
        def _():
            local = g - G_FDN
            fetch(ffn_down.at[aligned(local % 4, DM), aligned(local // 4, CW)])

    def ready(g):
        slot = g % NSLOT
        pltpu.make_async_copy(w_query.at[:, pl.ds(0, CW)], ring.at[slot], ring_sem.at[slot]).wait()
        return slot

    def done(g):
        start(g + NSLOT, g % NSLOT)

    def ag_copy(src, peer, index):
        return pltpu.make_async_remote_copy(toks.at[src], toks.at[src], ag_send.at[index], ag_recv.at[src], device_id={"ep": peer}, device_id_type=pl.DeviceIdType.MESH)

    def rt_copy(src, peer, index):
        return pltpu.make_async_remote_copy(route.at[src], route.at[src], rt_send.at[index], rt_recv.at[src], device_id={"ep": peer}, device_id_type=pl.DeviceIdType.MESH)

    def s0_copy(b):
        return pltpu.make_async_remote_copy(psib.at[b % 2], recv0.at[b], s0_send.at[b % 2], s0_recv.at[b], device_id={"ep": sib}, device_id_type=pl.DeviceIdType.MESH)

    def s1_copy(b, rel):
        return pltpu.make_async_remote_copy(pown.at[b, rel_chips[rel]], recv1.at[b, rel], s1_send.at[b, rel], s1_recv.at[b, rel], device_id={"ep": rel_chips[rel] * 2 + core}, device_id_type=pl.DeviceIdType.MESH)

    peers = tuple(c * 2 + core for c in rel_chips) + (sib,)

    for g in range(NSLOT):
        start(jnp.int32(g), g)
    barrier = pltpu.get_barrier_semaphore()
    for peer in peers:
        pl.semaphore_signal(barrier, inc=1, device_id={"ep": peer}, device_id_type=pl.DeviceIdType.MESH)

    hid_f = hid[...].astype(F32)
    inv_rms = lax.rsqrt(jnp.mean(hid_f * hid_f, axis=-1, keepdims=True) + RMS_EPS)
    for cb in range(NCB):
        part = hid[:, cb * CW:(cb + 1) * CW].astype(F32) * inv_rms
        toks[me, cb * TOK:(cb + 1) * TOK, :] = (part * moe_norm[:, cb * CW:(cb + 1) * CW].astype(F32)).astype(BF16)
        xn[:, cb * CW:(cb + 1) * CW] = (part * attn_norm[:, cb * CW:(cb + 1) * CW].astype(F32)).astype(BF16)

    logits = jnp.zeros((TOK, NEXP), F32)
    for cb in range(NCB):
        logits = logits + dot(toks[me, cb * TOK:(cb + 1) * TOK, :], w_router[cb * CW:(cb + 1) * CW, :])
    expert_iota = lax.broadcasted_iota(jnp.int32, (TOK, NEXP), 1)
    chosen = [jnp.sum(jnp.where(expert_iota == ids[:, j:j + 1], logits, 0.0), axis=-1, keepdims=True) for j in range(TOPK)]
    top = functools.reduce(jnp.maximum, chosen)
    raised = [jnp.exp(c - top) for c in chosen]
    total = functools.reduce(jnp.add, raised)
    pay[...] = jnp.zeros_like(pay)
    pay[:, 0:TOPK] = (ids[...] * CAP + slots[...]).astype(F32)
    for j in range(TOPK):
        pay[:, TOPK + j:TOPK + j + 1] = raised[j] / total
    route[me] = jnp.transpose(pay[...])[0:2 * TOPK, :]

    pl.semaphore_wait(barrier, 4)
    for index, peer in enumerate(peers):
        ag_copy(me, peer, index).start()

    row_i = lax.broadcasted_iota(jnp.int32, (TOK, TOK), 0)
    col_i = lax.broadcasted_iota(jnp.int32, (TOK, TOK), 1)
    causal = row_i >= col_i

    def rope_into(dst, vals):
        for h in range(CW // HEAD):
            part = vals[:, h * HEAD:(h + 1) * HEAD]
            turned = part * cos_t[...] + pltpu.roll(part, HEAD // 2, 1) * sin_t[...]
            dst[:, h * HEAD:(h + 1) * HEAD] = turned.astype(BF16)

    def attn_group(hg, carry):
        g = G_QKV + hg * 3
        slot = ready(g)
        rope_into(qs, dot(xn[...], ring[slot]))
        done(g)

        @pl.when(hg == 0)
        def _():
            for index, peer in enumerate(peers):
                rt_copy(me, peer, index).start()

        slot = ready(g + 1)
        rope_into(ks, dot(xn[...], ring[slot]))
        done(g + 1)
        slot = ready(g + 2)
        vs[...] = dot(xn[...], ring[slot]).astype(BF16)
        done(g + 2)
        for h in range(CW // HEAD):
            cols = slice(h * HEAD, (h + 1) * HEAD)
            scores = lax.dot_general(qs[:, cols], ks[:, cols], (((1,), (1,)), ((), ())), preferred_element_type=F32) * HEAD ** -0.5
            scores = jnp.where(causal, scores, -jnp.inf)
            expd = jnp.exp(scores - jnp.max(scores, axis=-1, keepdims=True))
            prob = (expd / jnp.sum(expd, axis=-1, keepdims=True)).astype(BF16)
            ctx[:, pl.ds(pl.multiple_of(hg * CW + h * HEAD, HEAD), HEAD)] = dot(prob, vs[:, cols]).astype(BF16)
        return carry

    lax.fori_loop(0, NCB, attn_group, 0)

    def out_block(n, carry):
        g = G_OUT + n
        slot = ready(g)
        cols = aligned(n, CW)
        a_s[:, cols] = (hid[:, cols].astype(F32) + dot(ctx[...], ring[slot])).astype(BF16)
        done(g)
        return carry

    lax.fori_loop(0, N_OUT, out_block, 0)
    xn[...] = rms(a_s[...].astype(F32), ffn_norm[...])

    def forward(rel):
        src = rel_chips[rel] * 2 + core
        ag_copy(src, sib, 4 + rel).wait_recv()
        ag_copy(src, sib, 4 + rel).start()
        rt_copy(src, sib, 4 + rel).wait_recv()
        rt_copy(src, sib, 4 + rel).start()

    forward(0)
    forward(1)

    def ffn_pair(g, col):
        slot = ready(g)
        z_gate = dot(xn[...], ring[slot])
        done(g)
        slot = ready(g + 1)
        z_up = dot(xn[...], ring[slot])
        done(g + 1)
        hff[:, aligned(col, CW)] = silu_mul(z_gate, z_up)

    def ffn_early(i, carry):
        ffn_pair(G_FFA + 2 * i, i)
        return carry

    lax.fori_loop(0, FF_EARLY, ffn_early, 0)

    forward(2)
    ag_copy(sib, sib, 0).wait_recv()
    rt_copy(sib, sib, 0).wait_recv()
    for rel in range(3):
        src = rel_chips[rel] * 2 + 1 - core
        ag_copy(src, sib, 0).wait_recv()
        rt_copy(src, sib, 0).wait_recv()

    def dispatch(src, carry):
        want = lax.broadcasted_iota(jnp.int32, (ROWS, TOK), 0).astype(F32) + (me * ROWS).astype(F32)
        pick = jnp.zeros((ROWS, TOK), F32)
        gate = jnp.zeros((ROWS, TOK), F32)
        for j in range(TOPK):
            hit = route[src, j:j + 1, :] == want
            pick = jnp.where(hit, 1.0, pick)
            gate = jnp.where(hit, route[src, TOPK + j:TOPK + j + 1, :], gate)
        gate_t = jnp.transpose(gate)
        high = gate_t.astype(BF16)
        rest = gate_t - high.astype(F32)
        mid = rest.astype(BF16)
        low = (rest - mid.astype(F32)).astype(BF16)
        gates[src, 0:TOK, :] = high
        gates[src, TOK:2 * TOK, :] = mid
        gates[src, 2 * TOK:3 * TOK, :] = low
        pick = pick.astype(BF16)
        for cb in range(NCB):
            rows = dot(pick, toks[src, cb * TOK:(cb + 1) * TOK, :]).astype(BF16)
            for e in range(LOCAL):
                disp[e, pl.ds(pl.multiple_of(src * CAP, 16), CAP), cb * CW:(cb + 1) * CW] = rows[e * CAP:(e + 1) * CAP, :]
        return carry

    lax.fori_loop(0, DEVS, dispatch, 0)

    for index, peer in enumerate(peers):
        ag_copy(me, peer, index).wait_send()
        rt_copy(me, peer, index).wait_send()
    for rel in range(3):
        src = rel_chips[rel] * 2 + core
        ag_copy(src, sib, 4 + rel).wait_send()
        rt_copy(src, sib, 4 + rel).wait_send()

    def expert_up(i, carry):
        g = G_EGU + 2 * i
        expert, col = i // 2, i % 2
        slot = ready(g)
        slot_up = ready(g + 1)
        for half in range(2):
            cols = slice(half * 256, (half + 1) * 256)
            z_gate = dot(disp[expert], ring[slot, :, cols])
            z_up = dot(disp[expert], ring[slot_up, :, cols])
            hexp[expert, :, pl.ds(pl.multiple_of(col * CW + half * 256, 256), 256)] = silu_mul(z_gate, z_up)
        done(g)
        done(g + 1)
        return carry

    lax.fori_loop(0, 2 * LOCAL, expert_up, 0)

    def fold(b):
        s0_copy(b).wait_recv()
        for c in range(4):
            pown[b, c] = pown[b, c] + recv0[b, c]

    def send1(b):
        for rel in range(3):
            s1_copy(b, rel).start()

    def down_block(b, carry):
        def down_pair(pair, inner):
            g = G_EDN + b * 4 + pair
            slot = ready(g)
            for i in range(2):
                e = pair * 2 + i
                y = dot(hexp[e], ring[slot, i * EFF:(i + 1) * EFF, :]).astype(BF16)
                for s in range(DEVS):
                    toks[s, pl.ds(pl.multiple_of(e * CAP, 16), CAP), :] = y[s * CAP:(s + 1) * CAP, :]
            done(g)

            @pl.when(jnp.logical_and(b >= 1, pair == 0))
            def _():
                s0_copy(b - 1).start()

            @pl.when(jnp.logical_and(b >= 1, pair == 2))
            def _():
                fold(b - 1)

            @pl.when(jnp.logical_and(b >= 1, pair == 3))
            def _():
                send1(b - 1)
            return inner

        lax.fori_loop(0, LOCAL // 2, down_pair, 0)

        @pl.when(b >= 2)
        def _():
            s0_copy(b - 2).wait_send()

        def combine(s):
            parts = dot(gates[s], toks[s, 0:ROWS, :])
            return parts[0:TOK] + parts[TOK:2 * TOK] + parts[2 * TOK:3 * TOK]

        def per_chip(c, inner):
            pown[b, c] = combine(c * 2 + core)
            psib[b % 2, c] = combine(c * 2 + 1 - core)
            return inner

        lax.fori_loop(0, 4, per_chip, 0)
        return carry

    lax.fori_loop(0, NCB, down_block, 0)

    def ffn_late(i, carry):
        ffn_pair(G_FFB + 2 * i, FF_EARLY + i)

        @pl.when(i == 0)
        def _():
            s0_copy(NCB - 1).start()

        @pl.when(i == 2)
        def _():
            fold(NCB - 1)

        @pl.when(i == 3)
        def _():
            send1(NCB - 1)
        return carry

    lax.fori_loop(0, FF // CW - FF_EARLY, ffn_late, 0)

    def down_out(n, carry):
        cols = aligned(n, CW)
        for kk in range(FF // DM):
            g = G_FDN + n * 4 + kk
            slot = ready(g)
            part = dot(hff[:, kk * DM:(kk + 1) * DM], ring[slot])
            if kk == 0:
                facc[...] = part
            else:
                facc[...] = facc[...] + part

            @pl.when(g + NSLOT < G_END)
            def _():
                done(g)
        for rel in range(3):
            s1_copy(n, rel).wait_recv()
        moe = pown[n, chip] + recv1[n, 0] + recv1[n, 1] + recv1[n, 2]
        out[:, cols] = (a_s[:, cols].astype(F32) + facc[...] + moe).astype(BF16)
        return carry

    lax.fori_loop(0, NCB, down_out, 0)

    for b in (NCB - 2, NCB - 1):
        s0_copy(b).wait_send()
    for b in range(NCB):
        for rel in range(3):
            s1_copy(b, rel).wait_send()


def rope_tables():
    half = HEAD // 2
    inv_freq = np.float32(ROPE_BASE) ** (np.float32(-2.0) * np.arange(half, dtype=np.float32) / np.float32(HEAD))
    angles = np.arange(TOK, dtype=np.float32)[:, None] * inv_freq[None, :].astype(np.float32)
    cos_h, sin_h = np.cos(angles).astype(np.float32), np.sin(angles).astype(np.float32)
    return np.concatenate([cos_h, cos_h], axis=1), np.concatenate([-sin_h, sin_h], axis=1)


def solution(mesh):
    row_spec = P(('dp', 'ep'), None, None)
    vec_spec = P(None)
    mat_spec = P(None, None)
    cube_spec = P(None, None, None)
    expert_spec = P('ep', None, None)
    vmem = pl.BlockSpec(memory_space=pltpu.VMEM)
    hbm = pl.BlockSpec(memory_space=pl.ANY)

    def per_device(hidden, expert_ids, slot_ids, attn_norm, w_query, w_key, w_value, w_out, ffn_norm, ffn_gate, ffn_up, ffn_down, moe_norm, w_router, exp_gate, exp_up, exp_down):
        cos_t, sin_t = rope_tables()
        dma = pltpu.SemaphoreType.DMA
        call = pl.pallas_call(
            kernel,
            out_shape=jax.ShapeDtypeStruct((TOK, DM), BF16),
            in_specs=[vmem] * 9 + [hbm] * 10,
            out_specs=vmem,
            scratch_shapes=[
                pltpu.VMEM((NSLOT, DM, CW), BF16),
                pltpu.VMEM((DEVS, NCB * TOK, CW), BF16),
                pltpu.VMEM((LOCAL, DEVS * CAP, DM), BF16),
                pltpu.VMEM((LOCAL, DEVS * CAP, EFF), BF16),
                pltpu.VMEM((NCB, 4, TOK, CW), F32),
                pltpu.VMEM((2, 4, TOK, CW), F32),
                pltpu.VMEM((NCB, 4, TOK, CW), F32),
                pltpu.VMEM((NCB, 3, TOK, CW), F32),
                pltpu.VMEM((DEVS, 3 * TOK, ROWS), BF16),
                pltpu.VMEM((DEVS, 2 * TOPK, TOK), F32),
                pltpu.VMEM((TOK, TOK), F32),
                pltpu.VMEM((TOK, DM), BF16),
                pltpu.VMEM((TOK, DM), BF16),
                pltpu.VMEM((TOK, DM), BF16),
                pltpu.VMEM((TOK, FF), BF16),
                pltpu.VMEM((TOK, CW), F32),
                pltpu.VMEM((TOK, CW), BF16),
                pltpu.VMEM((TOK, CW), BF16),
                pltpu.VMEM((TOK, CW), BF16),
                dma((NSLOT,)), dma((7,)), dma((DEVS,)), dma((7,)), dma((DEVS,)),
                dma((2,)), dma((NCB,)), dma((NCB, 3)), dma((NCB, 3)),
            ],
            compiler_params=pltpu.CompilerParams(collective_id=0, has_side_effects=True, vmem_limit_bytes=67043328),
            cost_estimate=pl.CostEstimate(flops=56_000_000_000, bytes_accessed=240_000_000, transcendentals=0),
        )
        res = call(
            hidden.reshape(TOK, DM), expert_ids.reshape(TOK, TOPK), slot_ids.reshape(TOK, TOPK),
            attn_norm.reshape(1, DM), ffn_norm.reshape(1, DM), moe_norm.reshape(1, DM), w_router, cos_t, sin_t,
            w_query, w_key, w_value, w_out.reshape(DM, DM), ffn_gate, ffn_up, ffn_down, exp_gate, exp_up, exp_down)
        return res.reshape(hidden.shape)

    return jax.shard_map(per_device, mesh=mesh, in_specs=(row_spec, row_spec, row_spec, vec_spec, mat_spec, mat_spec, mat_spec, cube_spec, vec_spec, mat_spec, mat_spec, mat_spec, vec_spec, mat_spec, expert_spec, expert_spec, expert_spec), out_specs=row_spec, check_vma=False)
```

time: 458 us -> 142 us (0.31)
  blocking collectives: 143 us -> 0 us
  matrix products: 140 us -> 0 us
  Pallas kernels: 0 us -> 131 us
  local copies, waits for them, and re-layouts: 79.8 us -> 10.5 us
  waiting for transfers between devices: 66.7 us -> 0 us
  other arithmetic: 19.1 us -> 0 us
    all_to_all x1 -> x0, blocking collectives: 143 us -> none  [per_device(): recv_buf = lax.all_to_all(send_buf, 'ep', 0, 1)]
    dot_general x11 -> x0, matrix products: 140 us -> none  [the longest x1 28.6 us: expert_ffn(): jnp.einsum('egcd,edf->egcf', expert_in, exp_gate, preferred_element_type=...]
    pallas_call x0 -> x1, Pallas kernels: none -> 131 us  [per_device(): call(hidden.reshape(TOK, DM), expert_ids.reshape(TOK, TOPK), slot_ids.res...]
    all_to_all x1 -> x0, waiting for transfers between devices: 66.7 us -> none  [per_device(): lax.all_to_all(expert_out, 'ep', 1, 0)]
    gather x6 -> x0, local copies, waits for them, and re-layouts: 38.6 us -> none  [the longest x1 16 us: per_device(): jnp.take(padded, owner_tok, axis=0)]
    dot_general x2 -> x0, local copies, waits for them, and re-layouts: 24.6 us -> none  [the longest x1 12.3 us: dense_branch(): jnp.einsum('bsd,de->bse', normed, w_query, preferred_element_type=jnp.flo...]
    broadcast_in_dim x2 -> x0, local copies, waits for them, and re-layouts: 10.9 us -> none  [the longest x1 10.8 us: per_device(): lax.all_to_all(expert_out, 'ep', 1, 0)]
    reduce_sum x5 -> x0, other arithmetic: 7.37 us -> none  [the longest x1 5.6 us: per_device(): jnp.sum(gate_vals[:, :, None] * picked.astype(jnp.float32), axis=1)]
  transfers between devices with their start and end apart: 1 -> 0, of which waited for: 1 -> 0; matrix products, arithmetic and copies ran while one was open for 16% -> 0% of each run, Pallas kernels for 0% -> 0%
where the time goes in v1:
time: 142 us; the launch traced here: 141 us
  Pallas kernels  131 us (92%)
  local copies, waits for them, and re-layouts  10.5 us (7%)
    pallas_call x1, Pallas kernels, per_device(): call(hidden.reshape(TOK, DM), expert_ids.reshape(TOK, TOPK), slot_ids.res...  131 us
    unnamed x4, local copies, waits for them, and re-layouts  6.64 us

profile of v1, /device:TPU:0, one launch (start us, length us, event | category | flops | bytes accessed | tf_op | source)
XLA Modules:
  0.0 141.2 jit_solution(1191910238646499938)
XLA Ops:
  0.0 1.3 reshape.27.attn_norm
  1.3 1.3 reshape.28.ffn_norm
  2.6 1.3 reshape.29.moe_norm
  3.8 1.4 copy.20
  5.2 1.4 copy.21
  6.6 2.0 %copy.22.w_router = bf16[2048,64]{1,0:T(8,128)(2,1)} copy(bf16[2048,64]{0,1:T(8,128)(2,1)} %param.32) | data formatting | bytes 524288 | tf_op args[13]
  8.6 130.7 %shard_map.181 = bf16[128,2048]{1,0:T(8,128)(2,1)} custom-call(bf16[128,2048]{1,0:T(8,128)(2,1)} %bitcast.7, s32[128,8]{1,0:T(8,128)} %bitcast.8, s32[128,8]{1,0:T(8,128)} %bitcast.9, bf16[1,2048]{1,0:T(2,128)(2,1)} %reshape.27.attn_norm, bf16[1,2048]{1,0:T(2,128)(2,1)} %reshape.28.ffn_norm, bf16[1,2048]{1,0:T(2,128)(2,1)} %reshape.29.moe_norm, ...), custom_call_target="tpu_custom_call" | custom-call | flops 56000000000 | bytes 240000000 | tf_op jit(solution)/shard_map/pallas_call | solution.py:476
  139.3 1.9 %copy.24 = bf16[1,128,2048]{2,1,0:T(8,128)(2,1)} copy(bf16[1,128,2048]{2,1,0:T(8,128)(2,1)} %bitcast.6) | data formatting | bytes 1048576

commit v2 on v1

--- a/solution.py
+++ b/solution.py
@@ -15,26 +15,29 @@
 
 DEVS = 8
 TOK = 128
+HALF = TOK // 2
 DM = 2048
 HEAD = 128
 FF = 8192
 LOCAL = 8
 EFF = 1024
 TOPK = 8
+LANE = 128
 CAP = 48
 ROWS = LOCAL * CAP
 NEXP = DEVS * LOCAL
 CW = 512
 NCB = DM // CW
 NSLOT = 8
-FF_EARLY = 6
+FF_EARLY = 5
 
 N_QKV = 12
 N_OUT = 4
 N_FFA = 2 * FF_EARLY
 N_EGU = 4 * LOCAL
 N_EDN = NCB * (LOCAL // 2)
-N_FFB = 2 * (FF // CW - FF_EARLY)
+N_LATE = FF // CW - FF_EARLY
+N_FFB = 2 * N_LATE
 N_FDN = NCB * (FF // DM)
 G_QKV = 0
 G_OUT = G_QKV + N_QKV
@@ -54,11 +57,6 @@
     return jnp.dot(lhs, rhs, preferred_element_type=F32)
 
 
-def rms(as_float, scale):
-    inv_rms = lax.rsqrt(jnp.mean(as_float * as_float, axis=-1, keepdims=True) + RMS_EPS)
-    return (as_float * inv_rms * scale.astype(F32)).astype(BF16)
-
-
 def silu_mul(z_gate, z_up):
     return (jax.nn.silu(z_gate) * z_up).astype(BF16)
 
@@ -66,13 +64,14 @@
 def kernel(hid, ids, slots, attn_norm, ffn_norm, moe_norm, w_router, cos_t, sin_t,
            w_query, w_key, w_value, w_out, ffn_gate, ffn_up, ffn_down, exp_gate, exp_up, exp_down,
            out,
-           ring, toks, disp, hexp, pown, psib, recv0, recv1, gates, route, pay, ctx, xn, a_s, hff, facc, qs, ks, vs,
-           ring_sem, ag_send, ag_recv, rt_send, rt_recv, s0_send, s0_recv, s1_send, s1_recv):
+           ring, toks, disp, hexp, pown, psib, recv0, recv1, recv2, gates, route, ctx, xn, a_s, hff, facc, qs, ks, vs, obuf,
+           ring_sem, ag_send, ag_recv, rt_send, rt_recv, s0_send, s0_recv, s1_send, s1_recv, s2_send, s2_recv, out_sem):
     me = lax.axis_index("ep")
     chip = me // 2
     core = me % 2
     sib = chip * 2 + 1 - core
-    rel_chips = (chip + 1 - 2 * (chip % 2), (chip + 2) % 4, 3 - chip)
+    chip_x, chip_y, chip_d = chip + 1 - 2 * (chip % 2), (chip + 2) % 4, 3 - chip
+    src_x, src_y, src_d = chip_x * 2 + core, chip_y * 2 + core, chip_d * 2 + core
 
     def start(g, slot):
         def fetch(src, rows=None):
@@ -146,50 +145,58 @@
     def done(g):
         start(g + NSLOT, g % NSLOT)
 
-    def ag_copy(src, peer, index):
-        return pltpu.make_async_remote_copy(toks.at[src], toks.at[src], ag_send.at[index], ag_recv.at[src], device_id={"ep": peer}, device_id_type=pl.DeviceIdType.MESH)
-
-    def rt_copy(src, peer, index):
-        return pltpu.make_async_remote_copy(route.at[src], route.at[src], rt_send.at[index], rt_recv.at[src], device_id={"ep": peer}, device_id_type=pl.DeviceIdType.MESH)
-
-    def s0_copy(b):
-        return pltpu.make_async_remote_copy(psib.at[b % 2], recv0.at[b], s0_send.at[b % 2], s0_recv.at[b], device_id={"ep": sib}, device_id_type=pl.DeviceIdType.MESH)
-
-    def s1_copy(b, rel):
-        return pltpu.make_async_remote_copy(pown.at[b, rel_chips[rel]], recv1.at[b, rel], s1_send.at[b, rel], s1_recv.at[b, rel], device_id={"ep": rel_chips[rel] * 2 + core}, device_id_type=pl.DeviceIdType.MESH)
-
-    peers = tuple(c * 2 + core for c in rel_chips) + (sib,)
+    def send(src, dst, send_sem, recv_sem, peer):
+        return pltpu.make_async_remote_copy(src, dst, send_sem, recv_sem, device_id={"ep": peer}, device_id_type=pl.DeviceIdType.MESH)
+
+    def ag_copy(src, cb, link):
+        block = toks.at[src, pl.ds(cb * TOK, TOK)]
+        return send(block, block, ag_send.at[link, src, cb], ag_recv.at[src, cb], (src_x, src_y, sib)[link])
+
+    def rt_copy(src, step):
+        return send(route.at[src], route.at[src], rt_send.at[step], rt_recv.at[src], (me + step) % DEVS)
+
+    def s0_copy(b, c):
+        return send(psib.at[b % 2, c], recv0.at[b, c], s0_send.at[b % 2, c], s0_recv.at[b, c], sib)
+
+    first_chip, first_dev = (chip_x, chip_y), (src_x, src_y)
+    second_chip, second_dev = (chip_y, chip_x), (src_y, src_x)
+
+    def s1_copy(b, half, which):
+        dest = first_chip[half] if which == 0 else chip_d
+        return send(pown.at[b, dest, pl.ds(half * HALF, HALF)], recv1.at[b, half, which], s1_send.at[b, half, which], s1_recv.at[b, half, which], first_dev[half])
+
+    def s2_copy(b, half):
+        return send(pown.at[b, second_chip[half], pl.ds(half * HALF, HALF)], recv2.at[b, half], s2_send.at[b, half], s2_recv.at[b, half], second_dev[half])
 
     for g in range(NSLOT):
         start(jnp.int32(g), g)
     barrier = pltpu.get_barrier_semaphore()
-    for peer in peers:
-        pl.semaphore_signal(barrier, inc=1, device_id={"ep": peer}, device_id_type=pl.DeviceIdType.MESH)
+    for step in range(1, DEVS):
+        pl.semaphore_signal(barrier, inc=1, device_id={"ep": (me + step) % DEVS}, device_id_type=pl.DeviceIdType.MESH)
 
     hid_f = hid[...].astype(F32)
     inv_rms = lax.rsqrt(jnp.mean(hid_f * hid_f, axis=-1, keepdims=True) + RMS_EPS)
+    for lt in range(DM // LANE):
+        cols = slice(lt * LANE, (lt + 1) * LANE)
+        cb, within_cb = divmod(lt * LANE, CW)
+        part = hid[:, cols].astype(F32) * inv_rms
+        toks[me, cb * TOK:(cb + 1) * TOK, within_cb:within_cb + LANE] = (part * moe_norm[lt:lt + 1, :].astype(F32)).astype(BF16)
+        xn[:, cols] = (part * attn_norm[lt:lt + 1, :].astype(F32)).astype(BF16)
+
+    logits = jnp.zeros((NEXP, TOK), F32)
     for cb in range(NCB):
-        part = hid[:, cb * CW:(cb + 1) * CW].astype(F32) * inv_rms
-        toks[me, cb * TOK:(cb + 1) * TOK, :] = (part * moe_norm[:, cb * CW:(cb + 1) * CW].astype(F32)).astype(BF16)
-        xn[:, cb * CW:(cb + 1) * CW] = (part * attn_norm[:, cb * CW:(cb + 1) * CW].astype(F32)).astype(BF16)
-
-    logits = jnp.zeros((TOK, NEXP), F32)
+        logits = logits + lax.dot_general(w_router[:, cb * CW:(cb + 1) * CW], toks[me, cb * TOK:(cb + 1) * TOK, :], (((1,), (1,)), ((), ())), preferred_element_type=F32)
+    expert_iota = lax.broadcasted_iota(jnp.int32, (NEXP, TOK), 0)
+    chosen = jnp.concatenate([jnp.sum(jnp.where(expert_iota == ids[j:j + 1, :], logits, 0.0), axis=0, keepdims=True) for j in range(TOPK)], axis=0)
+    raised = jnp.exp(chosen - jnp.max(chosen, axis=0, keepdims=True))
+    route[me, 0:TOPK, :] = (ids[...] * CAP + slots[...]).astype(F32)
+    route[me, TOPK:2 * TOPK, :] = raised / jnp.sum(raised, axis=0, keepdims=True)
+
+    pl.semaphore_wait(barrier, DEVS - 1)
     for cb in range(NCB):
-        logits = logits + dot(toks[me, cb * TOK:(cb + 1) * TOK, :], w_router[cb * CW:(cb + 1) * CW, :])
-    expert_iota = lax.broadcasted_iota(jnp.int32, (TOK, NEXP), 1)
-    chosen = [jnp.sum(jnp.where(expert_iota == ids[:, j:j + 1], logits, 0.0), axis=-1, keepdims=True) for j in range(TOPK)]
-    top = functools.reduce(jnp.maximum, chosen)
-    raised = [jnp.exp(c - top) for c in chosen]
-    total = functools.reduce(jnp.add, raised)
-    pay[...] = jnp.zeros_like(pay)
-    pay[:, 0:TOPK] = (ids[...] * CAP + slots[...]).astype(F32)
-    for j in range(TOPK):
-        pay[:, TOPK + j:TOPK + j + 1] = raised[j] / total
-    route[me] = jnp.transpose(pay[...])[0:2 * TOPK, :]
-
-    pl.semaphore_wait(barrier, 4)
-    for index, peer in enumerate(peers):
-        ag_copy(me, peer, index).start()
+        ag_copy(me, cb, 0).start()
+        ag_copy(me, (cb + 2) % NCB, 1).start()
+        ag_copy(me, cb, 2).start()
 
     row_i = lax.broadcasted_iota(jnp.int32, (TOK, TOK), 0)
     col_i = lax.broadcasted_iota(jnp.int32, (TOK, TOK), 1)
@@ -209,8 +216,8 @@
 
         @pl.when(hg == 0)
         def _():
-            for index, peer in enumerate(peers):
-                rt_copy(me, peer, index).start()
+            for step in range(1, DEVS):
+                rt_copy(me, step).start()
 
         slot = ready(g + 1)
         rope_into(ks, dot(xn[...], ring[slot]))
@@ -238,17 +245,20 @@
         return carry
 
     lax.fori_loop(0, N_OUT, out_block, 0)
-    xn[...] = rms(a_s[...].astype(F32), ffn_norm[...])
-
-    def forward(rel):
-        src = rel_chips[rel] * 2 + core
-        ag_copy(src, sib, 4 + rel).wait_recv()
-        ag_copy(src, sib, 4 + rel).start()
-        rt_copy(src, sib, 4 + rel).wait_recv()
-        rt_copy(src, sib, 4 + rel).start()
-
-    forward(0)
-    forward(1)
+    a_f = a_s[...].astype(F32)
+    inv_rms = lax.rsqrt(jnp.mean(a_f * a_f, axis=-1, keepdims=True) + RMS_EPS)
+    for lt in range(DM // LANE):
+        cols = slice(lt * LANE, (lt + 1) * LANE)
+        xn[:, cols] = (a_s[:, cols].astype(F32) * inv_rms * ffn_norm[lt:lt + 1, :].astype(F32)).astype(BF16)
+
+    def forward(src, cb, links):
+        ag_copy(src, cb, 2).wait_recv()
+        for link in links:
+            ag_copy(src, cb, link).start()
+
+    for cb in range(2):
+        forward(src_x, cb, (1, 2))
+        forward(src_y, cb + 2, (0, 2))
 
     def ffn_pair(g, col):
         slot = ready(g)
@@ -264,14 +274,6 @@
         return carry
 
     lax.fori_loop(0, FF_EARLY, ffn_early, 0)
-
-    forward(2)
-    ag_copy(sib, sib, 0).wait_recv()
-    rt_copy(sib, sib, 0).wait_recv()
-    for rel in range(3):
-        src = rel_chips[rel] * 2 + 1 - core
-        ag_copy(src, sib, 0).wait_recv()
-        rt_copy(src, sib, 0).wait_recv()
 
     def dispatch(src, carry):
         want = lax.broadcasted_iota(jnp.int32, (ROWS, TOK), 0).astype(F32) + (me * ROWS).astype(F32)
@@ -296,15 +298,40 @@
                 disp[e, pl.ds(pl.multiple_of(src * CAP, 16), CAP), cb * CW:(cb + 1) * CW] = rows[e * CAP:(e + 1) * CAP, :]
         return carry
 
-    lax.fori_loop(0, DEVS, dispatch, 0)
-
-    for index, peer in enumerate(peers):
-        ag_copy(me, peer, index).wait_send()
-        rt_copy(me, peer, index).wait_send()
-    for rel in range(3):
-        src = rel_chips[rel] * 2 + core
-        ag_copy(src, sib, 4 + rel).wait_send()
-        rt_copy(src, sib, 4 + rel).wait_send()
+    def arrived(src):
+        for cb in range(NCB):
+            ag_copy(src, cb, 2).wait_recv()
+
+    def dispatch_two(one, two):
+        lax.fori_loop(0, 2, lambda i, carry: dispatch(one + i * (two - one), carry), 0)
+
+    for step in range(1, DEVS):
+        rt_copy((me + step) % DEVS, step).wait_recv()
+    arrived(sib)
+    dispatch_two(me, sib)
+    for cb in range(2):
+        forward(src_x, cb + 2, (2,))
+        forward(src_y, cb, (2,))
+    dispatch_two(src_x, src_y)
+    sib_x, sib_y, sib_d = (c * 2 + 1 - core for c in (chip_x, chip_y, chip_d))
+    arrived(sib_x)
+    arrived(sib_y)
+    dispatch_two(sib_x, sib_y)
+    for cb in (0, 2, 1, 3):
+        forward(src_d, cb, (2,))
+    arrived(sib_d)
+    dispatch_two(src_d, sib_d)
+
+    for cb in range(NCB):
+        for link in range(3):
+            ag_copy(me, cb, link).wait_send()
+        for src in (src_x, src_y, src_d):
+            ag_copy(src, cb, 2).wait_send()
+    for cb in range(2):
+        ag_copy(src_x, cb, 1).wait_send()
+        ag_copy(src_y, cb + 2, 0).wait_send()
+    for step in range(1, DEVS):
+        rt_copy(me, step).wait_send()
 
     def expert_up(i, carry):
         g = G_EGU + 2 * i
@@ -322,14 +349,34 @@
 
     lax.fori_loop(0, 2 * LOCAL, expert_up, 0)
 
-    def fold(b):
-        s0_copy(b).wait_recv()
-        for c in range(4):
-            pown[b, c] = pown[b, c] + recv0[b, c]
+    def fold(b, c):
+        s0_copy(b, c).wait_recv()
+        pown[b, c] = pown[b, c] + recv0[b, c]
+
+    def fold_others(b):
+        s0_copy(b, chip).start()
+        for c in (chip_d, chip_x, chip_y):
+            fold(b, c)
+
+    def send1_fold_own(b):
+        send1(b)
+        fold(b, chip)
 
     def send1(b):
-        for rel in range(3):
-            s1_copy(b, rel).start()
+        for which in (1, 0):
+            for half in range(2):
+                s1_copy(b, half, which).start()
+
+    def fold1(b):
+        for half in range(2):
+            rows = slice(half * HALF, (half + 1) * HALF)
+            for which, dest in ((1, second_chip[half]), (0, chip)):
+                s1_copy(b, half, which).wait_recv()
+                pown[b, dest, rows, :] = pown[b, dest, rows, :] + recv1[b, half, which]
+
+    def send2(b):
+        for half in range(2):
+            s2_copy(b, half).start()
 
     def down_block(b, carry):
         def down_pair(pair, inner):
@@ -342,35 +389,41 @@
                     toks[s, pl.ds(pl.multiple_of(e * CAP, 16), CAP), :] = y[s * CAP:(s + 1) * CAP, :]
             done(g)
 
-            @pl.when(jnp.logical_and(b >= 1, pair == 0))
-            def _():
-                s0_copy(b - 1).start()
-
-            @pl.when(jnp.logical_and(b >= 1, pair == 2))
-            def _():
-                fold(b - 1)
-
-            @pl.when(jnp.logical_and(b >= 1, pair == 3))
-            def _():
-                send1(b - 1)
+            def at(first, step):
+                return pl.when(jnp.logical_and(b >= first, pair == step))
+
+            @at(1, 0)
+            def _():
+                fold_others(b - 1)
+
+            @at(1, 1)
+            def _():
+                send1_fold_own(b - 1)
+
+            @at(2, 3)
+            def _():
+                fold1(b - 2)
             return inner
 
         lax.fori_loop(0, LOCAL // 2, down_pair, 0)
-
-        @pl.when(b >= 2)
-        def _():
-            s0_copy(b - 2).wait_send()
 
         def combine(s):
             parts = dot(gates[s], toks[s, 0:ROWS, :])
             return parts[0:TOK] + parts[TOK:2 * TOK] + parts[2 * TOK:3 * TOK]
 
-        def per_chip(c, inner):
+        @pl.when(b >= 2)
+        def _():
+            send2(b - 2)
+            for c in range(4):
+                s0_copy(b - 2, c).wait_send()
+
+        last = None
+        for c in (chip_d, chip_x, chip_y, chip):
+            psib[b % 2, c] = combine(c * 2 + 1 - core)
+            if last is not None:
+                s0_copy(b, last).start()
             pown[b, c] = combine(c * 2 + core)
-            psib[b % 2, c] = combine(c * 2 + 1 - core)
-            return inner
-
-        lax.fori_loop(0, 4, per_chip, 0)
+            last = c
         return carry
 
     lax.fori_loop(0, NCB, down_block, 0)
@@ -378,20 +431,17 @@
     def ffn_late(i, carry):
         ffn_pair(G_FFB + 2 * i, FF_EARLY + i)
 
-        @pl.when(i == 0)
-        def _():
-            s0_copy(NCB - 1).start()
-
-        @pl.when(i == 2)
-        def _():
-            fold(NCB - 1)
-
-        @pl.when(i == 3)
-        def _():
-            send1(NCB - 1)
-        return carry
-
-    lax.fori_loop(0, FF // CW - FF_EARLY, ffn_late, 0)
+        for step, act in (
+                (0, lambda: fold_others(NCB - 1)), (1, lambda: send1_fold_own(NCB - 1)), (2, lambda: fold1(NCB - 2)),
+                (3, lambda: send2(NCB - 2)), (N_LATE - 2, lambda: fold1(NCB - 1)), (N_LATE - 1, lambda: send2(NCB - 1))):
+            pl.when(i == step)(act)
+        return carry
+
+    lax.fori_loop(0, N_LATE, ffn_late, 0)
+
+    def out_copy(n):
+        cols = aligned(n, CW)
+        return pltpu.make_async_copy(obuf.at[:, cols], out.at[:, cols], out_sem.at[n])
 
     def down_out(n, carry):
         cols = aligned(n, CW)
@@ -404,22 +454,31 @@
             else:
                 facc[...] = facc[...] + part
 
-            @pl.when(g + NSLOT < G_END)
-            def _():
-                done(g)
-        for rel in range(3):
-            s1_copy(n, rel).wait_recv()
-        moe = pown[n, chip] + recv1[n, 0] + recv1[n, 1] + recv1[n, 2]
-        out[:, cols] = (a_s[:, cols].astype(F32) + facc[...] + moe).astype(BF16)
+            done(g)
+            if kk == 1:
+                @pl.when(n > 0)
+                def _():
+                    out_copy(n - 1).start()
+        for half in range(2):
+            rows = slice(half * HALF, (half + 1) * HALF)
+            s2_copy(n, half).wait_recv()
+            moe = pown[n, chip, rows, :] + recv2[n, half]
+            obuf[rows, cols] = (a_s[rows, cols].astype(F32) + facc[rows, :] + moe).astype(BF16)
         return carry
 
     lax.fori_loop(0, NCB, down_out, 0)
 
+    for b in range(NCB):
+        for half in range(2):
+            s1_copy(b, half, 0).wait_send()
+            s1_copy(b, half, 1).wait_send()
+            s2_copy(b, half).wait_send()
     for b in (NCB - 2, NCB - 1):
-        s0_copy(b).wait_send()
-    for b in range(NCB):
-        for rel in range(3):
-            s1_copy(b, rel).wait_send()
+        for c in range(4):
+            s0_copy(b, c).wait_send()
+    out_copy(NCB - 1).start()
+    for n in range(NCB):
+        out_copy(n).wait()
 
 
 def rope_tables():
@@ -446,7 +505,7 @@
             kernel,
             out_shape=jax.ShapeDtypeStruct((TOK, DM), BF16),
             in_specs=[vmem] * 9 + [hbm] * 10,
-            out_specs=vmem,
+            out_specs=hbm,
             scratch_shapes=[
                 pltpu.VMEM((NSLOT, DM, CW), BF16),
                 pltpu.VMEM((DEVS, NCB * TOK, CW), BF16),
@@ -455,10 +514,10 @@
                 pltpu.VMEM((NCB, 4, TOK, CW), F32),
                 pltpu.VMEM((2, 4, TOK, CW), F32),
                 pltpu.VMEM((NCB, 4, TOK, CW), F32),
-                pltpu.VMEM((NCB, 3, TOK, CW), F32),
+                pltpu.VMEM((NCB, 2, 2, HALF, CW), F32),
+                pltpu.VMEM((NCB, 2, HALF, CW), F32),
                 pltpu.VMEM((DEVS, 3 * TOK, ROWS), BF16),
                 pltpu.VMEM((DEVS, 2 * TOPK, TOK), F32),
-                pltpu.VMEM((TOK, TOK), F32),
                 pltpu.VMEM((TOK, DM), BF16),
                 pltpu.VMEM((TOK, DM), BF16),
                 pltpu.VMEM((TOK, DM), BF16),
@@ -467,15 +526,16 @@
                 pltpu.VMEM((TOK, CW), BF16),
                 pltpu.VMEM((TOK, CW), BF16),
                 pltpu.VMEM((TOK, CW), BF16),
-                dma((NSLOT,)), dma((7,)), dma((DEVS,)), dma((7,)), dma((DEVS,)),
-                dma((2,)), dma((NCB,)), dma((NCB, 3)), dma((NCB, 3)),
+                pltpu.VMEM((TOK, DM), BF16),
+                dma((NSLOT,)), dma((3, DEVS, NCB)), dma((DEVS, NCB)), dma((DEVS,)), dma((DEVS,)),
+                dma((2, 4)), dma((NCB, 4)), dma((NCB, 2, 2)), dma((NCB, 2, 2)), dma((NCB, 2)), dma((NCB, 2)), dma((NCB,)),
             ],
             compiler_params=pltpu.CompilerParams(collective_id=0, has_side_effects=True, vmem_limit_bytes=67043328),
             cost_estimate=pl.CostEstimate(flops=56_000_000_000, bytes_accessed=240_000_000, transcendentals=0),
         )
         res = call(
-            hidden.reshape(TOK, DM), expert_ids.reshape(TOK, TOPK), slot_ids.reshape(TOK, TOPK),
-            attn_norm.reshape(1, DM), ffn_norm.reshape(1, DM), moe_norm.reshape(1, DM), w_router, cos_t, sin_t,
+            hidden.reshape(TOK, DM), expert_ids.reshape(TOK, TOPK).T, slot_ids.reshape(TOK, TOPK).T,
+            attn_norm.reshape(DM // LANE, LANE), ffn_norm.reshape(DM // LANE, LANE), moe_norm.reshape(DM // LANE, LANE), w_router.T, cos_t, sin_t,
             w_query, w_key, w_value, w_out.reshape(DM, DM), ffn_gate, ffn_up, ffn_down, exp_gate, exp_up, exp_down)
         return res.reshape(hidden.shape)
 

time: 142 us -> 112 us (0.79)
  Pallas kernels: 131 us -> 110 us
  local copies, waits for them, and re-layouts: 10.5 us -> 1.88 us
    pallas_call x1, Pallas kernels: 131 us -> 110 us  [per_device(): call(hidden.reshape(TOK, DM), expert_ids.reshape(TOK, TOPK).T, slot_ids.r...]
    unnamed x4 -> x1, local copies, waits for them, and re-layouts: 6.64 us -> 1.88 us
    reshape x3 -> x0, local copies, waits for them, and re-layouts: 3.84 us -> none  [the longest x1 1.29 us: per_device(): ffn_norm.reshape(1, DM)]
where the time goes in v2:
time: 112 us
  Pallas kernels  110 us (98%)
  local copies, waits for them, and re-layouts  1.88 us (2%)
    pallas_call x1, Pallas kernels, per_device(): call(hidden.reshape(TOK, DM), expert_ids.reshape(TOK, TOPK).T, slot_ids.r...  110 us

profile of v2, /device:TPU:0, one launch (start us, length us, event | category | flops | bytes accessed | tf_op | source)
XLA Modules:
  0.0 111.7 jit_solution(17052534725295481734)
XLA Ops:
  0.0 109.8 %shard_map.181 = bf16[128,2048]{1,0:T(8,128)(2,1)} custom-call(bf16[128,2048]{1,0:T(8,128)(2,1)} %bitcast.15, s32[8,128]{1,0:T(8,128)} %bitcast.17, s32[8,128]{1,0:T(8,128)} %bitcast.18, bf16[16,128]{1,0:T(8,128)(2,1)} %bitcast.19, bf16[16,128]{1,0:T(8,128)(2,1)} %bitcast.20, bf16[16,128]{1,0:T(8,128)(2,1)} %bitcast.21, bf16[64,2048]{1,0:T(8,128)(2,1)} %bitcast.16, ...), custom_call_target="tpu_custom_call" | custom-call | flops 56000000000 | bytes 240000000 | tf_op jit(solution)/shard_map/pallas_call | solution.py:536
  109.8 1.9 %copy.21 = bf16[1,128,2048]{2,1,0:T(8,128)(2,1)} copy(bf16[1,128,2048]{2,1,0:T(8,128)(2,1)} %bitcast.14) | data formatting | bytes 1048576

commit v3 on v2

--- a/solution.py
+++ b/solution.py
@@ -20,6 +20,7 @@
 HEAD = 128
 FF = 8192
 LOCAL = 8
+FOLD1_AT = ((3, 0), (4, 1), (6, 2), (7, 3))
 EFF = 1024
 TOPK = 8
 LANE = 128
@@ -28,17 +29,22 @@
 NEXP = DEVS * LOCAL
 CW = 512
 NCB = DM // CW
+BW = 256
+NBW = DM // BW
+FF_PAIRS = FF // 2 // CW
 NSLOT = 8
-FF_EARLY = 5
+FF_EARLY = 1
+FF_MID = 0
 
 N_QKV = 12
 N_OUT = 4
-N_FFA = 2 * FF_EARLY
+N_FFA = 2 * (FF_EARLY + FF_MID)
 N_EGU = 4 * LOCAL
-N_EDN = NCB * (LOCAL // 2)
-N_LATE = FF // CW - FF_EARLY
+N_EDN = NBW * (LOCAL // 4)
+N_LATE = FF_PAIRS - FF_EARLY - FF_MID
 N_FFB = 2 * N_LATE
-N_FDN = NCB * (FF // DM)
+N_FK = FF // 2 // DM
+N_FDN = NCB * N_FK
 G_QKV = 0
 G_OUT = G_QKV + N_QKV
 G_FFA = G_OUT + N_OUT
@@ -64,8 +70,8 @@
 def kernel(hid, ids, slots, attn_norm, ffn_norm, moe_norm, w_router, cos_t, sin_t,
            w_query, w_key, w_value, w_out, ffn_gate, ffn_up, ffn_down, exp_gate, exp_up, exp_down,
            out,
-           ring, toks, disp, hexp, pown, psib, recv0, recv1, recv2, gates, route, ctx, xn, a_s, hff, facc, qs, ks, vs, obuf,
-           ring_sem, ag_send, ag_recv, rt_send, rt_recv, s0_send, s0_recv, s1_send, s1_recv, s2_send, s2_recv, out_sem):
+           ring, toks, disp, hexp, pown, psib, recv0, recv1, recv2, gates, route, ctx, xn, xx, fsend, frecv, a_s, hff, facc, qs, ks, vs, obuf,
+           ring_sem, ag_send, ag_recv, rt_send, rt_recv, s0_send, s0_recv, s1_send, s1_recv, s2_send, s2_recv, x_send, x_recv, f_send, f_recv, out_sem):
     me = lax.axis_index("ep")
     chip = me // 2
     core = me % 2
@@ -74,8 +80,8 @@
     src_x, src_y, src_d = chip_x * 2 + core, chip_y * 2 + core, chip_d * 2 + core
 
     def start(g, slot):
-        def fetch(src, rows=None):
-            dst = ring.at[slot] if rows is None else ring.at[slot, rows]
+        def fetch(src, part=None):
+            dst = ring.at[slot] if part is None else ring.at[(slot,) + part]
             pltpu.make_async_copy(src, dst, ring_sem.at[slot]).start()
 
         def within(lo, hi):
@@ -94,7 +100,7 @@
             fetch(w_out.at[:, aligned(g - G_OUT, CW)])
 
         def ff_pair(local, first):
-            col, kind = first + local // 2, local % 2
+            col, kind = core * FF_PAIRS + first + local // 2, local % 2
 
             @pl.when(kind == 0)
             def _():
@@ -124,18 +130,18 @@
         @within(G_EDN, G_FFB)
         def _():
             local = g - G_EDN
-            col, pair = local // 4, local % 4
-            for i in range(2):
-                fetch(exp_down.at[pair * 2 + i, :, aligned(col, CW)], pl.ds(i * EFF, EFF))
+            col, quad = local // 2, local % 2
+            for i in range(4):
+                fetch(exp_down.at[quad * 4 + i, :, aligned(col, BW)], (pl.ds(i // 2 * EFF, EFF), pl.ds(i % 2 * BW, BW)))
 
         @within(G_FFB, G_FDN)
         def _():
-            ff_pair(g - G_FFB, FF_EARLY)
+            ff_pair(g - G_FFB, FF_EARLY + FF_MID)
 
         @within(G_FDN, G_END)
         def _():
             local = g - G_FDN
-            fetch(ffn_down.at[aligned(local % 4, DM), aligned(local // 4, CW)])
+            fetch(ffn_down.at[aligned(core * N_FK + local % N_FK, DM), aligned(local // N_FK, CW)])
 
     def ready(g):
         slot = g % NSLOT
@@ -155,18 +161,18 @@
     def rt_copy(src, step):
         return send(route.at[src], route.at[src], rt_send.at[step], rt_recv.at[src], (me + step) % DEVS)
 
-    def s0_copy(b, c):
-        return send(psib.at[b % 2, c], recv0.at[b, c], s0_send.at[b % 2, c], s0_recv.at[b, c], sib)
-
-    first_chip, first_dev = (chip_x, chip_y), (src_x, src_y)
-    second_chip, second_dev = (chip_y, chip_x), (src_y, src_x)
-
-    def s1_copy(b, half, which):
-        dest = first_chip[half] if which == 0 else chip_d
-        return send(pown.at[b, dest, pl.ds(half * HALF, HALF)], recv1.at[b, half, which], s1_send.at[b, half, which], s1_recv.at[b, half, which], first_dev[half])
+    first_dev, second_dev = (src_x, src_y), (src_y, src_x)
+    slot_of = {"own": (0, 0), "x": (2, 1), "y": (1, 2), "d": (3, 3)}
+
+    def s0_copy(b, half, late):
+        part = pl.ds(0 if late else 2, 2)
+        return send(psib.at[b % 2, half, part], recv0.at[b, half, part], s0_send.at[b % 2, half, int(late)], s0_recv.at[b, half, int(late)], sib)
+
+    def s1_copy(b, half):
+        return send(pown.at[b, half, pl.ds(2, 2)], recv1.at[b, half], s1_send.at[b, half], s1_recv.at[b, half], first_dev[half])
 
     def s2_copy(b, half):
-        return send(pown.at[b, second_chip[half], pl.ds(half * HALF, HALF)], recv2.at[b, half], s2_send.at[b, half], s2_recv.at[b, half], second_dev[half])
+        return send(pown.at[b, half, 1], recv2.at[b, half], s2_send.at[b, half], s2_recv.at[b, half], second_dev[half])
 
     for g in range(NSLOT):
         start(jnp.int32(g), g)
@@ -183,6 +189,12 @@
         toks[me, cb * TOK:(cb + 1) * TOK, within_cb:within_cb + LANE] = (part * moe_norm[lt:lt + 1, :].astype(F32)).astype(BF16)
         xn[:, cols] = (part * attn_norm[lt:lt + 1, :].astype(F32)).astype(BF16)
 
+    pl.semaphore_wait(barrier, DEVS - 1)
+    for cb in range(NCB):
+        ag_copy(me, cb, 0).start()
+        ag_copy(me, (cb + 2) % NCB, 1).start()
+        ag_copy(me, cb, 2).start()
+
     logits = jnp.zeros((NEXP, TOK), F32)
     for cb in range(NCB):
         logits = logits + lax.dot_general(w_router[:, cb * CW:(cb + 1) * CW], toks[me, cb * TOK:(cb + 1) * TOK, :], (((1,), (1,)), ((), ())), preferred_element_type=F32)
@@ -192,11 +204,10 @@
     route[me, 0:TOPK, :] = (ids[...] * CAP + slots[...]).astype(F32)
     route[me, TOPK:2 * TOPK, :] = raised / jnp.sum(raised, axis=0, keepdims=True)
 
-    pl.semaphore_wait(barrier, DEVS - 1)
-    for cb in range(NCB):
-        ag_copy(me, cb, 0).start()
-        ag_copy(me, (cb + 2) % NCB, 1).start()
-        ag_copy(me, cb, 2).start()
+    def forward(src, cb, links):
+        ag_copy(src, cb, 2).wait_recv()
+        for link in links:
+            ag_copy(src, cb, link).start()
 
     row_i = lax.broadcasted_iota(jnp.int32, (TOK, TOK), 0)
     col_i = lax.broadcasted_iota(jnp.int32, (TOK, TOK), 1)
@@ -232,6 +243,11 @@
             expd = jnp.exp(scores - jnp.max(scores, axis=-1, keepdims=True))
             prob = (expd / jnp.sum(expd, axis=-1, keepdims=True)).astype(BF16)
             ctx[:, pl.ds(pl.multiple_of(hg * CW + h * HEAD, HEAD), HEAD)] = dot(prob, vs[:, cols]).astype(BF16)
+
+        @pl.when(hg >= 2)
+        def _():
+            forward(src_x, hg - 2, (1, 2))
+            forward(src_y, hg, (0, 2))
         return carry
 
     lax.fori_loop(0, NCB, attn_group, 0)
@@ -249,31 +265,24 @@
     inv_rms = lax.rsqrt(jnp.mean(a_f * a_f, axis=-1, keepdims=True) + RMS_EPS)
     for lt in range(DM // LANE):
         cols = slice(lt * LANE, (lt + 1) * LANE)
-        xn[:, cols] = (a_s[:, cols].astype(F32) * inv_rms * ffn_norm[lt:lt + 1, :].astype(F32)).astype(BF16)
-
-    def forward(src, cb, links):
-        ag_copy(src, cb, 2).wait_recv()
-        for link in links:
-            ag_copy(src, cb, link).start()
-
-    for cb in range(2):
-        forward(src_x, cb, (1, 2))
-        forward(src_y, cb + 2, (0, 2))
+        xx[aligned(core, TOK), cols] = (a_s[:, cols].astype(F32) * inv_rms * ffn_norm[lt:lt + 1, :].astype(F32)).astype(BF16)
+    x_block = xx.at[aligned(core, TOK)]
+    x_copy = send(x_block, x_block, x_send, x_recv, sib)
 
     def ffn_pair(g, col):
         slot = ready(g)
-        z_gate = dot(xn[...], ring[slot])
+        slot_up = ready(g + 1)
+        for half in range(2):
+            cols = slice(half * 256, (half + 1) * 256)
+            z_gate = dot(xx[...], ring[slot, :, cols])
+            z_up = dot(xx[...], ring[slot_up, :, cols])
+            hff[:, pl.ds(pl.multiple_of(col * CW + half * 256, 256), 256)] = silu_mul(z_gate, z_up)
         done(g)
-        slot = ready(g + 1)
-        z_up = dot(xn[...], ring[slot])
         done(g + 1)
-        hff[:, aligned(col, CW)] = silu_mul(z_gate, z_up)
 
     def ffn_early(i, carry):
         ffn_pair(G_FFA + 2 * i, i)
         return carry
-
-    lax.fori_loop(0, FF_EARLY, ffn_early, 0)
 
     def dispatch(src, carry):
         want = lax.broadcasted_iota(jnp.int32, (ROWS, TOK), 0).astype(F32) + (me * ROWS).astype(F32)
@@ -309,16 +318,22 @@
         rt_copy((me + step) % DEVS, step).wait_recv()
     arrived(sib)
     dispatch_two(me, sib)
+    x_copy.start()
     for cb in range(2):
         forward(src_x, cb + 2, (2,))
         forward(src_y, cb, (2,))
     dispatch_two(src_x, src_y)
+    x_copy.wait()
+    lax.fori_loop(0, FF_EARLY, ffn_early, 0)
     sib_x, sib_y, sib_d = (c * 2 + 1 - core for c in (chip_x, chip_y, chip_d))
     arrived(sib_x)
     arrived(sib_y)
+    for cb in (0, 2):
+        forward(src_d, cb, (2,))
     dispatch_two(sib_x, sib_y)
-    for cb in (0, 2, 1, 3):
+    for cb in (1, 3):
         forward(src_d, cb, (2,))
+    lax.fori_loop(FF_EARLY, FF_EARLY + FF_MID, ffn_early, 0)
     arrived(sib_d)
     dispatch_two(src_d, sib_d)
 
@@ -333,107 +348,99 @@
     for step in range(1, DEVS):
         rt_copy(me, step).wait_send()
 
-    def expert_up(i, carry):
-        g = G_EGU + 2 * i
-        expert, col = i // 2, i % 2
-        slot = ready(g)
-        slot_up = ready(g + 1)
-        for half in range(2):
-            cols = slice(half * 256, (half + 1) * 256)
-            z_gate = dot(disp[expert], ring[slot, :, cols])
-            z_up = dot(disp[expert], ring[slot_up, :, cols])
-            hexp[expert, :, pl.ds(pl.multiple_of(col * CW + half * 256, 256), 256)] = silu_mul(z_gate, z_up)
-        done(g)
-        done(g + 1)
-        return carry
-
-    lax.fori_loop(0, 2 * LOCAL, expert_up, 0)
-
-    def fold(b, c):
-        s0_copy(b, c).wait_recv()
-        pown[b, c] = pown[b, c] + recv0[b, c]
-
-    def fold_others(b):
-        s0_copy(b, chip).start()
-        for c in (chip_d, chip_x, chip_y):
-            fold(b, c)
-
-    def send1_fold_own(b):
-        send1(b)
-        fold(b, chip)
+    def expert_up(expert, carry):
+        g = G_EGU + 4 * expert
+        held = [ready(g + i) for i in range(4)]
+        for quarter in range(2):
+            z_gate = dot(disp[expert], ring[held[quarter * 2]])
+            z_up = dot(disp[expert], ring[held[quarter * 2 + 1]])
+            hexp[expert, :, quarter * 512:(quarter + 1) * 512] = silu_mul(z_gate, z_up)
+        for i in range(4):
+            done(g + i)
+        return carry
+
+    lax.fori_loop(0, LOCAL, expert_up, 0)
+
+    def fold0(b, late):
+        for half in range(2):
+            s0_copy(b, half, late).wait_recv()
+            part = slice(0, 2) if late else slice(2, 4)
+            pown[b, half, part] = pown[b, half, part] + recv0[b, half, part]
+
+    def start0(b, late):
+        for half in range(2):
+            s0_copy(b, half, late).start()
 
     def send1(b):
-        for which in (1, 0):
+        for half in range(2):
+            s1_copy(b, half).start()
+
+    def fold1(b):
+        for half in range(2):
+            s1_copy(b, half).wait_recv()
+            pown[b, half, 0:2] = pown[b, half, 0:2] + recv1[b, half]
+
+    def send2(b):
+        for half in range(2):
+            s2_copy(b, half).start()
+
+    def down_block(b, carry):
+        def down_quad(quad):
+            g = G_EDN + b * 2 + quad
+            slot = ready(g)
+            for i in range(4):
+                e = quad * 4 + i
+                y = dot(hexp[e], ring[slot, i // 2 * EFF:(i // 2 + 1) * EFF, i % 2 * BW:(i % 2 + 1) * BW]).astype(BF16)
+                for s in range(DEVS):
+                    toks[s, e * CAP:(e + 1) * CAP, 0:BW] = y[s * CAP:(s + 1) * CAP, :]
+            done(g)
+
+        def combine(dest, side):
+            for name, c in (("d", chip_d), ("x", chip_x), ("y", chip_y), ("own", chip)):
+                parts = dot(gates[c * 2 + side], toks[c * 2 + side, 0:ROWS, 0:BW])
+                moe = parts[0:TOK] + parts[TOK:2 * TOK] + parts[2 * TOK:3 * TOK]
+                for half in range(2):
+                    dest[half, slot_of[name][half]] = moe[half * HALF:(half + 1) * HALF]
+
+        down_quad(0)
+
+        @pl.when(b >= 1)
+        def _():
+            fold0(b - 1, False)
+
+        for step, block in FOLD1_AT:
+            pl.when(b == step)(functools.partial(fold1, block))
+
+        @pl.when(b >= 2)
+        def _():
             for half in range(2):
-                s1_copy(b, half, which).start()
-
-    def fold1(b):
-        for half in range(2):
-            rows = slice(half * HALF, (half + 1) * HALF)
-            for which, dest in ((1, second_chip[half]), (0, chip)):
-                s1_copy(b, half, which).wait_recv()
-                pown[b, dest, rows, :] = pown[b, dest, rows, :] + recv1[b, half, which]
-
-    def send2(b):
-        for half in range(2):
-            s2_copy(b, half).start()
-
-    def down_block(b, carry):
-        def down_pair(pair, inner):
-            g = G_EDN + b * 4 + pair
-            slot = ready(g)
-            for i in range(2):
-                e = pair * 2 + i
-                y = dot(hexp[e], ring[slot, i * EFF:(i + 1) * EFF, :]).astype(BF16)
-                for s in range(DEVS):
-                    toks[s, pl.ds(pl.multiple_of(e * CAP, 16), CAP), :] = y[s * CAP:(s + 1) * CAP, :]
-            done(g)
-
-            def at(first, step):
-                return pl.when(jnp.logical_and(b >= first, pair == step))
-
-            @at(1, 0)
-            def _():
-                fold_others(b - 1)
-
-            @at(1, 1)
-            def _():
-                send1_fold_own(b - 1)
-
-            @at(2, 3)
-            def _():
-                fold1(b - 2)
-            return inner
-
-        lax.fori_loop(0, LOCAL // 2, down_pair, 0)
-
-        def combine(s):
-            parts = dot(gates[s], toks[s, 0:ROWS, :])
-            return parts[0:TOK] + parts[TOK:2 * TOK] + parts[2 * TOK:3 * TOK]
-
-        @pl.when(b >= 2)
-        def _():
-            send2(b - 2)
-            for c in range(4):
-                s0_copy(b - 2, c).wait_send()
-
-        last = None
-        for c in (chip_d, chip_x, chip_y, chip):
-            psib[b % 2, c] = combine(c * 2 + 1 - core)
-            if last is not None:
-                s0_copy(b, last).start()
-            pown[b, c] = combine(c * 2 + core)
-            last = c
-        return carry
-
-    lax.fori_loop(0, NCB, down_block, 0)
+                s0_copy(b - 2, half, False).wait_send()
+                s0_copy(b - 2, half, True).wait_send()
+
+        down_quad(1)
+
+        @pl.when(b >= 1)
+        def _():
+            send1(b - 1)
+            fold0(b - 1, True)
+
+        for step, block in FOLD1_AT:
+            pl.when(b == step)(functools.partial(send2, block))
+
+        combine(psib.at[b % 2], 1 - core)
+        start0(b, False)
+        combine(pown.at[b], core)
+        start0(b, True)
+        return carry
+
+    lax.fori_loop(0, NBW, down_block, 0)
 
     def ffn_late(i, carry):
-        ffn_pair(G_FFB + 2 * i, FF_EARLY + i)
+        ffn_pair(G_FFB + 2 * i, FF_EARLY + FF_MID + i)
 
         for step, act in (
-                (0, lambda: fold_others(NCB - 1)), (1, lambda: send1_fold_own(NCB - 1)), (2, lambda: fold1(NCB - 2)),
-                (3, lambda: send2(NCB - 2)), (N_LATE - 2, lambda: fold1(NCB - 1)), (N_LATE - 1, lambda: send2(NCB - 1))):
+                (0, lambda: fold0(NBW - 1, False)), (1, lambda: send1(NBW - 1)), (1, lambda: fold1(4)),
+                (2, lambda: fold0(NBW - 1, True)), (2, lambda: send2(4)), (3, lambda: fold1(5)), (4, lambda: send2(5)), (5, lambda: fold1(6)), (6, lambda: send2(6))):
             pl.when(i == step)(act)
         return carry
 
@@ -443,40 +450,65 @@
         cols = aligned(n, CW)
         return pltpu.make_async_copy(obuf.at[:, cols], out.at[:, cols], out_sem.at[n])
 
-    def down_out(n, carry):
-        cols = aligned(n, CW)
-        for kk in range(FF // DM):
-            g = G_FDN + n * 4 + kk
+    def f_copy(n):
+        return send(fsend.at[n], frecv.at[n], f_send.at[n], f_recv.at[n], sib)
+
+    def ffn_out(n, carry):
+        for kk in range(N_FK):
+            g = G_FDN + n * N_FK + kk
             slot = ready(g)
             part = dot(hff[:, kk * DM:(kk + 1) * DM], ring[slot])
+            done(g)
             if kk == 0:
                 facc[...] = part
             else:
                 facc[...] = facc[...] + part
-
-            done(g)
-            if kk == 1:
-                @pl.when(n > 0)
-                def _():
-                    out_copy(n - 1).start()
-        for half in range(2):
-            rows = slice(half * HALF, (half + 1) * HALF)
-            s2_copy(n, half).wait_recv()
-            moe = pown[n, chip, rows, :] + recv2[n, half]
-            obuf[rows, cols] = (a_s[rows, cols].astype(F32) + facc[rows, :] + moe).astype(BF16)
-        return carry
-
-    lax.fori_loop(0, NCB, down_out, 0)
-
-    for b in range(NCB):
-        for half in range(2):
-            s1_copy(b, half, 0).wait_send()
-            s1_copy(b, half, 1).wait_send()
-            s2_copy(b, half).wait_send()
-    for b in (NCB - 2, NCB - 1):
-        for c in range(4):
-            s0_copy(b, c).wait_send()
-    out_copy(NCB - 1).start()
+        fsend[n] = facc[aligned(1 - core, TOK), :]
+        for w in range(CW // BW):
+            b = n * (CW // BW) + w
+            for half in range(2):
+                mine = facc[pl.ds(pl.multiple_of(core * TOK + half * HALF, HALF), HALF), w * BW:(w + 1) * BW]
+                pown[b, half, 0] = pown[b, half, 0] + mine
+        pl.when(n >= 1)(lambda: f_copy(n - 1).start())
+        for step, act in ((0, lambda: fold1(7)), (1, lambda: send2(7))):
+            pl.when(n == step)(act)
+        return carry
+
+    lax.fori_loop(0, NCB, ffn_out, 0)
+
+    def final(n):
+        f_copy(n).wait_recv()
+        for w in range(CW // BW):
+            b = n * (CW // BW) + w
+            cols = slice(b * BW, (b + 1) * BW)
+            for half in range(2):
+                rows = slice(half * HALF, (half + 1) * HALF)
+                s2_copy(b, half).wait_recv()
+                total = pown[b, half, 0] + recv2[b, half] + frecv[n, rows, w * BW:(w + 1) * BW]
+                obuf[rows, cols] = (a_s[rows, cols].astype(F32) + total).astype(BF16)
+
+    final(0)
+    f_copy(NCB - 1).start()
+    final(1)
+    out_copy(0).start()
+    final(2)
+    out_copy(1).start()
+    for b in range(NBW):
+        for half in range(2):
+            s1_copy(b, half).wait_send()
+            if b < NBW - 1:
+                s2_copy(b, half).wait_send()
+    for b in (NBW - 2, NBW - 1):
+        for half in range(2):
+            s0_copy(b, half, False).wait_send()
+            s0_copy(b, half, True).wait_send()
+    for n in range(NCB):
+        f_copy(n).wait_send()
+    out_copy(2).start()
+    final(3)
+    for half in range(2):
+        s2_copy(NBW - 1, half).wait_send()
+    out_copy(3).start()
     for n in range(NCB):
         out_copy(n).wait()
 
@@ -511,24 +543,28 @@
                 pltpu.VMEM((DEVS, NCB * TOK, CW), BF16),
                 pltpu.VMEM((LOCAL, DEVS * CAP, DM), BF16),
                 pltpu.VMEM((LOCAL, DEVS * CAP, EFF), BF16),
-                pltpu.VMEM((NCB, 4, TOK, CW), F32),
-                pltpu.VMEM((2, 4, TOK, CW), F32),
-                pltpu.VMEM((NCB, 4, TOK, CW), F32),
-                pltpu.VMEM((NCB, 2, 2, HALF, CW), F32),
-                pltpu.VMEM((NCB, 2, HALF, CW), F32),
+                pltpu.VMEM((NBW, 2, 4, HALF, BW), F32),
+                pltpu.VMEM((2, 2, 4, HALF, BW), F32),
+                pltpu.VMEM((NBW, 2, 4, HALF, BW), F32),
+                pltpu.VMEM((NBW, 2, 2, HALF, BW), F32),
+                pltpu.VMEM((NBW, 2, HALF, BW), F32),
                 pltpu.VMEM((DEVS, 3 * TOK, ROWS), BF16),
                 pltpu.VMEM((DEVS, 2 * TOPK, TOK), F32),
                 pltpu.VMEM((TOK, DM), BF16),
                 pltpu.VMEM((TOK, DM), BF16),
+                pltpu.VMEM((2 * TOK, DM), BF16),
+                pltpu.VMEM((NCB, TOK, CW), F32),
+                pltpu.VMEM((NCB, TOK, CW), F32),
                 pltpu.VMEM((TOK, DM), BF16),
-                pltpu.VMEM((TOK, FF), BF16),
-                pltpu.VMEM((TOK, CW), F32),
+                pltpu.VMEM((2 * TOK, FF // 2), BF16),
+                pltpu.VMEM((2 * TOK, CW), F32),
                 pltpu.VMEM((TOK, CW), BF16),
                 pltpu.VMEM((TOK, CW), BF16),
                 pltpu.VMEM((TOK, CW), BF16),
                 pltpu.VMEM((TOK, DM), BF16),
                 dma((NSLOT,)), dma((3, DEVS, NCB)), dma((DEVS, NCB)), dma((DEVS,)), dma((DEVS,)),
-                dma((2, 4)), dma((NCB, 4)), dma((NCB, 2, 2)), dma((NCB, 2, 2)), dma((NCB, 2)), dma((NCB, 2)), dma((NCB,)),
+                dma((2, 2, 2)), dma((NBW, 2, 2)), dma((NBW, 2)), dma((NBW, 2)), dma((NBW, 2)), dma((NBW, 2)),
+                dma(()), dma(()), dma((NCB,)), dma((NCB,)), dma((NCB,)),
             ],
             compiler_params=pltpu.CompilerParams(collective_id=0, has_side_effects=True, vmem_limit_bytes=67043328),
             cost_estimate=pl.CostEstimate(flops=56_000_000_000, bytes_accessed=240_000_000, transcendentals=0),

time: 112 us -> 104 us (0.929)
  Pallas kernels: 110 us -> 102 us
    pallas_call x1, Pallas kernels: 110 us -> 102 us  [per_device(): call(hidden.reshape(TOK, DM), expert_ids.reshape(TOK, TOPK).T, slot_ids.r...]
where the time goes in v3:
time: 104 us
  Pallas kernels  102 us (98%)
  local copies, waits for them, and re-layouts  1.88 us (2%)
    pallas_call x1, Pallas kernels, per_device(): call(hidden.reshape(TOK, DM), expert_ids.reshape(TOK, TOPK).T, slot_ids.r...  102 us

profile of v3, /device:TPU:0, one launch (start us, length us, event | category | flops | bytes accessed | tf_op | source)
XLA Modules:
  0.0 103.5 jit_solution(16003218786170119537)
XLA Ops:
  0.0 101.6 %shard_map.181 = bf16[128,2048]{1,0:T(8,128)(2,1)} custom-call(bf16[128,2048]{1,0:T(8,128)(2,1)} %bitcast.15, s32[8,128]{1,0:T(8,128)} %bitcast.17, s32[8,128]{1,0:T(8,128)} %bitcast.18, bf16[16,128]{1,0:T(8,128)(2,1)} %bitcast.19, bf16[16,128]{1,0:T(8,128)(2,1)} %bitcast.20, bf16[16,128]{1,0:T(8,128)(2,1)} %bitcast.21, bf16[64,2048]{1,0:T(8,128)(2,1)} %bitcast.16, ...), custom_call_target="tpu_custom_call" | custom-call | flops 56000000000 | bytes 240000000 | tf_op jit(solution)/shard_map/pallas_call | solution.py:572
  101.6 1.9 %copy.21 = bf16[1,128,2048]{2,1,0:T(8,128)(2,1)} copy(bf16[1,128,2048]{2,1,0:T(8,128)(2,1)} %bitcast.14) | data formatting | bytes 1048576

commit v4 on v3

--- a/solution.py
+++ b/solution.py
@@ -70,13 +70,14 @@
 def kernel(hid, ids, slots, attn_norm, ffn_norm, moe_norm, w_router, cos_t, sin_t,
            w_query, w_key, w_value, w_out, ffn_gate, ffn_up, ffn_down, exp_gate, exp_up, exp_down,
            out,
-           ring, toks, disp, hexp, pown, psib, recv0, recv1, recv2, gates, route, ctx, xn, xx, fsend, frecv, a_s, hff, facc, qs, ks, vs, obuf,
-           ring_sem, ag_send, ag_recv, rt_send, rt_recv, s0_send, s0_recv, s1_send, s1_recv, s2_send, s2_recv, x_send, x_recv, f_send, f_recv, out_sem):
+           ring, toks, disp, hexp, pown, psib, recv0, recv1, recv2, gates, route, ctx, xx, fsend, frecv, a_s, hff, facc, qs, ks, vs,
+           ring_sem, ag_send, ag_recv, rt_send, rt_recv, s0_send, s0_recv, s1_send, s1_recv, s2_send, s2_recv, x_send, x_recv, f_send, f_recv):
     me = lax.axis_index("ep")
     chip = me // 2
     core = me % 2
     sib = chip * 2 + 1 - core
     chip_x, chip_y, chip_d = chip + 1 - 2 * (chip % 2), (chip + 2) % 4, 3 - chip
+    mine = aligned(core, TOK)
     src_x, src_y, src_d = chip_x * 2 + core, chip_y * 2 + core, chip_d * 2 + core
 
     def start(g, slot):
@@ -154,25 +155,35 @@
     def send(src, dst, send_sem, recv_sem, peer):
         return pltpu.make_async_remote_copy(src, dst, send_sem, recv_sem, device_id={"ep": peer}, device_id_type=pl.DeviceIdType.MESH)
 
-    def ag_copy(src, cb, link):
+    def ag_copy(src, cb, link, sem):
         block = toks.at[src, pl.ds(cb * TOK, TOK)]
-        return send(block, block, ag_send.at[link, src, cb], ag_recv.at[src, cb], (src_x, src_y, sib)[link])
+        return send(block, block, ag_send.at[0], ag_recv.at[sem], (src_x, src_y, sib)[link])
+
+    def ag_wait(blocks, sem):
+        block = toks.at[0, pl.ds(0, blocks * TOK)]
+        send(block, block, ag_send.at[0], ag_recv.at[sem], sib).wait_recv()
 
     def rt_copy(src, step):
-        return send(route.at[src], route.at[src], rt_send.at[step], rt_recv.at[src], (me + step) % DEVS)
+        return send(route.at[src], route.at[src], rt_send.at[0], rt_recv.at[0], (me + step) % DEVS)
 
     first_dev, second_dev = (src_x, src_y), (src_y, src_x)
     slot_of = {"own": (0, 0), "x": (2, 1), "y": (1, 2), "d": (3, 3)}
 
     def s0_copy(b, half, late):
         part = pl.ds(0 if late else 2, 2)
-        return send(psib.at[b % 2, half, part], recv0.at[b, half, part], s0_send.at[b % 2, half, int(late)], s0_recv.at[b, half, int(late)], sib)
+        return send(psib.at[b % 2, half, part], recv0.at[b % 4, half, part], s0_send.at[b % 2], s0_recv.at[b, int(late)], sib)
 
     def s1_copy(b, half):
-        return send(pown.at[b, half, pl.ds(2, 2)], recv1.at[b, half], s1_send.at[b, half], s1_recv.at[b, half], first_dev[half])
+        return send(pown.at[b, half, pl.ds(2, 2)], recv1.at[b, half], s1_send.at[0], s1_recv.at[b], first_dev[half])
 
     def s2_copy(b, half):
-        return send(pown.at[b, half, 1], recv2.at[b, half], s2_send.at[b, half], s2_recv.at[b, half], second_dev[half])
+        return send(pown.at[b, half, 1], recv2.at[b, half], s2_send.at[0], s2_recv.at[b], second_dev[half])
+
+    def wait_sent(block, sem):
+        send(block, block, sem, s2_recv.at[0], sib).wait_send()
+
+    def wait_got(block, sem):
+        send(block, block, s2_send.at[0], sem, sib).wait_recv()
 
     for g in range(NSLOT):
         start(jnp.int32(g), g)
@@ -187,13 +198,13 @@
         cb, within_cb = divmod(lt * LANE, CW)
         part = hid[:, cols].astype(F32) * inv_rms
         toks[me, cb * TOK:(cb + 1) * TOK, within_cb:within_cb + LANE] = (part * moe_norm[lt:lt + 1, :].astype(F32)).astype(BF16)
-        xn[:, cols] = (part * attn_norm[lt:lt + 1, :].astype(F32)).astype(BF16)
+        xx[mine, cols] = (part * attn_norm[lt:lt + 1, :].astype(F32)).astype(BF16)
 
     pl.semaphore_wait(barrier, DEVS - 1)
     for cb in range(NCB):
-        ag_copy(me, cb, 0).start()
-        ag_copy(me, (cb + 2) % NCB, 1).start()
-        ag_copy(me, cb, 2).start()
+        ag_copy(me, cb, 0, min(cb, 2)).start()
+        ag_copy(me, (cb + 2) % NCB, 1, 3 + min(cb, 2)).start()
+        ag_copy(me, cb, 2, 8).start()
 
     logits = jnp.zeros((NEXP, TOK), F32)
     for cb in range(NCB):
@@ -204,10 +215,16 @@
     route[me, 0:TOPK, :] = (ids[...] * CAP + slots[...]).astype(F32)
     route[me, TOPK:2 * TOPK, :] = raised / jnp.sum(raised, axis=0, keepdims=True)
 
-    def forward(src, cb, links):
-        ag_copy(src, cb, 2).wait_recv()
-        for link in links:
-            ag_copy(src, cb, link).start()
+    def relay(cb, sem_x, sem_y, sem_d):
+        for src, block, link, sem, sem_sib in ((src_x, cb, 1, sem_x, 9), (src_y, cb + 2, 0, sem_y, 10)):
+            ag_wait(1, sem)
+            ag_copy(src, block, link, sem_d).start()
+            ag_copy(src, block, 2, sem_sib).start()
+
+    def forward(src, blocks, sem, sem_sib):
+        ag_wait(2, sem)
+        for cb in blocks:
+            ag_copy(src, cb, 2, sem_sib).start()
 
     row_i = lax.broadcasted_iota(jnp.int32, (TOK, TOK), 0)
     col_i = lax.broadcasted_iota(jnp.int32, (TOK, TOK), 1)
@@ -222,7 +239,7 @@
     def attn_group(hg, carry):
         g = G_QKV + hg * 3
         slot = ready(g)
-        rope_into(qs, dot(xn[...], ring[slot]))
+        rope_into(qs, dot(xx[mine], ring[slot]))
         done(g)
 
         @pl.when(hg == 0)
@@ -231,10 +248,10 @@
                 rt_copy(me, step).start()
 
         slot = ready(g + 1)
-        rope_into(ks, dot(xn[...], ring[slot]))
+        rope_into(ks, dot(xx[mine], ring[slot]))
         done(g + 1)
         slot = ready(g + 2)
-        vs[...] = dot(xn[...], ring[slot]).astype(BF16)
+        vs[...] = dot(xx[mine], ring[slot]).astype(BF16)
         done(g + 2)
         for h in range(CW // HEAD):
             cols = slice(h * HEAD, (h + 1) * HEAD)
@@ -244,10 +261,13 @@
             prob = (expd / jnp.sum(expd, axis=-1, keepdims=True)).astype(BF16)
             ctx[:, pl.ds(pl.multiple_of(hg * CW + h * HEAD, HEAD), HEAD)] = dot(prob, vs[:, cols]).astype(BF16)
 
-        @pl.when(hg >= 2)
-        def _():
-            forward(src_x, hg - 2, (1, 2))
-            forward(src_y, hg, (0, 2))
+        @pl.when(hg == 2)
+        def _():
+            relay(0, 0, 3, 6)
+
+        @pl.when(hg == 3)
+        def _():
+            relay(1, 1, 4, 7)
         return carry
 
     lax.fori_loop(0, NCB, attn_group, 0)
@@ -272,11 +292,9 @@
     def ffn_pair(g, col):
         slot = ready(g)
         slot_up = ready(g + 1)
-        for half in range(2):
-            cols = slice(half * 256, (half + 1) * 256)
-            z_gate = dot(xx[...], ring[slot, :, cols])
-            z_up = dot(xx[...], ring[slot_up, :, cols])
-            hff[:, pl.ds(pl.multiple_of(col * CW + half * 256, 256), 256)] = silu_mul(z_gate, z_up)
+        z_gate = dot(xx[...], ring[slot])
+        z_up = dot(xx[...], ring[slot_up])
+        hff[:, aligned(col, CW)] = silu_mul(z_gate, z_up)
         done(g)
         done(g + 1)
 
@@ -307,46 +325,30 @@
                 disp[e, pl.ds(pl.multiple_of(src * CAP, 16), CAP), cb * CW:(cb + 1) * CW] = rows[e * CAP:(e + 1) * CAP, :]
         return carry
 
-    def arrived(src):
-        for cb in range(NCB):
-            ag_copy(src, cb, 2).wait_recv()
-
     def dispatch_two(one, two):
         lax.fori_loop(0, 2, lambda i, carry: dispatch(one + i * (two - one), carry), 0)
 
-    for step in range(1, DEVS):
-        rt_copy((me + step) % DEVS, step).wait_recv()
-    arrived(sib)
+    wait_got(route.at[pl.ds(0, DEVS - 1)], rt_recv.at[0])
+    ag_wait(4, 8)
     dispatch_two(me, sib)
     x_copy.start()
-    for cb in range(2):
-        forward(src_x, cb + 2, (2,))
-        forward(src_y, cb, (2,))
+    forward(src_x, (2, 3), 2, 9)
+    forward(src_y, (0, 1), 5, 10)
     dispatch_two(src_x, src_y)
     x_copy.wait()
     lax.fori_loop(0, FF_EARLY, ffn_early, 0)
     sib_x, sib_y, sib_d = (c * 2 + 1 - core for c in (chip_x, chip_y, chip_d))
-    arrived(sib_x)
-    arrived(sib_y)
-    for cb in (0, 2):
-        forward(src_d, cb, (2,))
+    ag_wait(4, 9)
+    ag_wait(4, 10)
+    forward(src_d, (0, 2), 6, 11)
     dispatch_two(sib_x, sib_y)
-    for cb in (1, 3):
-        forward(src_d, cb, (2,))
+    forward(src_d, (1, 3), 7, 11)
     lax.fori_loop(FF_EARLY, FF_EARLY + FF_MID, ffn_early, 0)
-    arrived(sib_d)
+    ag_wait(4, 11)
     dispatch_two(src_d, sib_d)
 
-    for cb in range(NCB):
-        for link in range(3):
-            ag_copy(me, cb, link).wait_send()
-        for src in (src_x, src_y, src_d):
-            ag_copy(src, cb, 2).wait_send()
-    for cb in range(2):
-        ag_copy(src_x, cb, 1).wait_send()
-        ag_copy(src_y, cb + 2, 0).wait_send()
-    for step in range(1, DEVS):
-        rt_copy(me, step).wait_send()
+    wait_sent(toks.at[pl.ds(0, 7)], ag_send.at[0])
+    wait_sent(route.at[pl.ds(0, DEVS - 1)], rt_send.at[0])
 
     def expert_up(expert, carry):
         g = G_EGU + 4 * expert
@@ -362,10 +364,10 @@
     lax.fori_loop(0, LOCAL, expert_up, 0)
 
     def fold0(b, late):
+        wait_got(recv0.at[0, 0], s0_recv.at[b, int(late)])
         for half in range(2):
-            s0_copy(b, half, late).wait_recv()
             part = slice(0, 2) if late else slice(2, 4)
-            pown[b, half, part] = pown[b, half, part] + recv0[b, half, part]
+            pown[b, half, part] = pown[b, half, part] + recv0[b % 4, half, part]
 
     def start0(b, late):
         for half in range(2):
@@ -376,8 +378,8 @@
             s1_copy(b, half).start()
 
     def fold1(b):
+        wait_got(recv1.at[b], s1_recv.at[b])
         for half in range(2):
-            s1_copy(b, half).wait_recv()
             pown[b, half, 0:2] = pown[b, half, 0:2] + recv1[b, half]
 
     def send2(b):
@@ -413,9 +415,7 @@
 
         @pl.when(b >= 2)
         def _():
-            for half in range(2):
-                s0_copy(b - 2, half, False).wait_send()
-                s0_copy(b - 2, half, True).wait_send()
+            wait_sent(psib.at[b % 2], s0_send.at[b % 2])
 
         down_quad(1)
 
@@ -446,12 +446,8 @@
 
     lax.fori_loop(0, N_LATE, ffn_late, 0)
 
-    def out_copy(n):
-        cols = aligned(n, CW)
-        return pltpu.make_async_copy(obuf.at[:, cols], out.at[:, cols], out_sem.at[n])
-
     def f_copy(n):
-        return send(fsend.at[n], frecv.at[n], f_send.at[n], f_recv.at[n], sib)
+        return send(fsend.at[n], frecv.at[n], f_send.at[0], f_recv.at[n], sib)
 
     def ffn_out(n, carry):
         for kk in range(N_FK):
@@ -467,8 +463,8 @@
         for w in range(CW // BW):
             b = n * (CW // BW) + w
             for half in range(2):
-                mine = facc[pl.ds(pl.multiple_of(core * TOK + half * HALF, HALF), HALF), w * BW:(w + 1) * BW]
-                pown[b, half, 0] = pown[b, half, 0] + mine
+                own = facc[pl.ds(pl.multiple_of(core * TOK + half * HALF, HALF), HALF), w * BW:(w + 1) * BW]
+                pown[b, half, 0] = pown[b, half, 0] + own
         pl.when(n >= 1)(lambda: f_copy(n - 1).start())
         for step, act in ((0, lambda: fold1(7)), (1, lambda: send2(7))):
             pl.when(n == step)(act)
@@ -481,36 +477,22 @@
         for w in range(CW // BW):
             b = n * (CW // BW) + w
             cols = slice(b * BW, (b + 1) * BW)
+            wait_got(recv2.at[b], s2_recv.at[b])
             for half in range(2):
                 rows = slice(half * HALF, (half + 1) * HALF)
-                s2_copy(b, half).wait_recv()
                 total = pown[b, half, 0] + recv2[b, half] + frecv[n, rows, w * BW:(w + 1) * BW]
-                obuf[rows, cols] = (a_s[rows, cols].astype(F32) + total).astype(BF16)
+                out[rows, cols] = (a_s[rows, cols].astype(F32) + total).astype(BF16)
 
     final(0)
     f_copy(NCB - 1).start()
     final(1)
-    out_copy(0).start()
     final(2)
-    out_copy(1).start()
-    for b in range(NBW):
-        for half in range(2):
-            s1_copy(b, half).wait_send()
-            if b < NBW - 1:
-                s2_copy(b, half).wait_send()
-    for b in (NBW - 2, NBW - 1):
-        for half in range(2):
-            s0_copy(b, half, False).wait_send()
-            s0_copy(b, half, True).wait_send()
-    for n in range(NCB):
-        f_copy(n).wait_send()
-    out_copy(2).start()
+    wait_sent(pown.at[pl.ds(0, 4)], s1_send.at[0])
+    for parity in range(2):
+        wait_sent(psib.at[parity], s0_send.at[parity])
+    wait_sent(fsend, f_send.at[0])
     final(3)
-    for half in range(2):
-        s2_copy(NBW - 1, half).wait_send()
-    out_copy(3).start()
-    for n in range(NCB):
-        out_copy(n).wait()
+    wait_sent(pown.at[pl.ds(0, 2)], s2_send.at[0])
 
 
 def rope_tables():
@@ -535,9 +517,9 @@
         dma = pltpu.SemaphoreType.DMA
         call = pl.pallas_call(
             kernel,
-            out_shape=jax.ShapeDtypeStruct((TOK, DM), BF16),
+            out_shape=pltpu.VMEM((TOK, DM), BF16),
             in_specs=[vmem] * 9 + [hbm] * 10,
-            out_specs=hbm,
+            out_specs=vmem,
             scratch_shapes=[
                 pltpu.VMEM((NSLOT, DM, CW), BF16),
                 pltpu.VMEM((DEVS, NCB * TOK, CW), BF16),
@@ -545,12 +527,11 @@
                 pltpu.VMEM((LOCAL, DEVS * CAP, EFF), BF16),
                 pltpu.VMEM((NBW, 2, 4, HALF, BW), F32),
                 pltpu.VMEM((2, 2, 4, HALF, BW), F32),
-                pltpu.VMEM((NBW, 2, 4, HALF, BW), F32),
+                pltpu.VMEM((4, 2, 4, HALF, BW), F32),
                 pltpu.VMEM((NBW, 2, 2, HALF, BW), F32),
                 pltpu.VMEM((NBW, 2, HALF, BW), F32),
                 pltpu.VMEM((DEVS, 3 * TOK, ROWS), BF16),
                 pltpu.VMEM((DEVS, 2 * TOPK, TOK), F32),
-                pltpu.VMEM((TOK, DM), BF16),
                 pltpu.VMEM((TOK, DM), BF16),
                 pltpu.VMEM((2 * TOK, DM), BF16),
                 pltpu.VMEM((NCB, TOK, CW), F32),
@@ -561,12 +542,11 @@
                 pltpu.VMEM((TOK, CW), BF16),
                 pltpu.VMEM((TOK, CW), BF16),
                 pltpu.VMEM((TOK, CW), BF16),
-                pltpu.VMEM((TOK, DM), BF16),
-                dma((NSLOT,)), dma((3, DEVS, NCB)), dma((DEVS, NCB)), dma((DEVS,)), dma((DEVS,)),
-                dma((2, 2, 2)), dma((NBW, 2, 2)), dma((NBW, 2)), dma((NBW, 2)), dma((NBW, 2)), dma((NBW, 2)),
-                dma(()), dma(()), dma((NCB,)), dma((NCB,)), dma((NCB,)),
+                dma((NSLOT,)), dma((1,)), dma((12,)), dma((1,)), dma((1,)),
+                dma((2,)), dma((NBW, 2)), dma((1,)), dma((NBW,)), dma((1,)), dma((NBW,)),
+                dma(()), dma(()), dma((1,)), dma((NCB,)),
             ],
-            compiler_params=pltpu.CompilerParams(collective_id=0, has_side_effects=True, vmem_limit_bytes=67043328),
+            compiler_params=pltpu.CompilerParams(collective_id=0, has_side_effects=True, vmem_limit_bytes=66000000),
             cost_estimate=pl.CostEstimate(flops=56_000_000_000, bytes_accessed=240_000_000, transcendentals=0),
         )
         res = call(

time: 104 us -> 99.9 us (0.961)
  Pallas kernels: 102 us -> 99 us
  local copies, waits for them, and re-layouts: 1.88 us -> 0.8 us
    pallas_call x1, Pallas kernels: 102 us -> 99 us  [per_device(): call(hidden.reshape(TOK, DM), expert_ids.reshape(TOK, TOPK).T, slot_ids.r...]
    unnamed x1, local copies, waits for them, and re-layouts: 1.88 us -> 0.8 us
where the time goes in v4:
time: 99.9 us; the launch traced here: 99.8 us
  Pallas kernels  99 us (99%)
    pallas_call x1, Pallas kernels, per_device(): call(hidden.reshape(TOK, DM), expert_ids.reshape(TOK, TOPK).T, slot_ids.r...  99 us

profile of v4, /device:TPU:0, one launch (start us, length us, event | category | flops | bytes accessed | tf_op | source)
XLA Modules:
  0.0 99.8 jit_solution(11450707327200114819)
XLA Ops:
  0.0 99.0 %shard_map.181 = bf16[128,2048]{1,0:T(8,128)(2,1)S(1)} custom-call(bf16[128,2048]{1,0:T(8,128)(2,1)} %bitcast.15, s32[8,128]{1,0:T(8,128)} %bitcast.17, s32[8,128]{1,0:T(8,128)} %bitcast.18, bf16[16,128]{1,0:T(8,128)(2,1)} %bitcast.19, bf16[16,128]{1,0:T(8,128)(2,1)} %bitcast.20, bf16[16,128]{1,0:T(8,128)(2,1)} %bitcast.21, bf16[64,2048]{1,0:T(8,128)(2,1)} %bitcast.16, ...), custom_call_target="tpu_custom_call" | custom-call | flops 56000000000 | bytes 240000000 | tf_op jit(solution)/shard_map/pallas_call | solution.py:552
  99.0 0.8 copy.21

commit v5 on v4

--- a/solution.py
+++ b/solution.py
@@ -20,7 +20,9 @@
 HEAD = 128
 FF = 8192
 LOCAL = 8
-FOLD1_AT = ((3, 0), (4, 1), (6, 2), (7, 3))
+FOLD1_MID = ((5, 2),)
+FOLD1_END = ((2, 0), (3, 1), (6, 3), (7, 4))
+SEND2_START = ((3, 0), (4, 1), (7, 3))
 EFF = 1024
 TOPK = 8
 LANE = 128
@@ -67,11 +69,12 @@
     return (jax.nn.silu(z_gate) * z_up).astype(BF16)
 
 
-def kernel(hid, ids, slots, attn_norm, ffn_norm, moe_norm, w_router, cos_t, sin_t,
+def kernel(hid_h, ids_h, slots_h, attn_norm_h, ffn_norm_h, moe_norm_h, w_router_h, cos_h, sin_h,
            w_query, w_key, w_value, w_out, ffn_gate, ffn_up, ffn_down, exp_gate, exp_up, exp_down,
            out,
-           ring, toks, disp, hexp, pown, psib, recv0, recv1, recv2, gates, route, ctx, xx, fsend, frecv, a_s, hff, facc, qs, ks, vs,
-           ring_sem, ag_send, ag_recv, rt_send, rt_recv, s0_send, s0_recv, s1_send, s1_recv, s2_send, s2_recv, x_send, x_recv, f_send, f_recv):
+           ring, toks, disp, hexp, pown, psib, recv0, recv1, recv2, gates, picks, route, ctx, xx, fsend, frecv, a_s, hff, facc, qs, ks, vs,
+           ring_sem, ag_send, ag_recv, rt_send, rt_recv, s0_send, s0_recv, s1_send, s1_recv, s2_send, s2_recv, x_send, x_recv, f_send, f_recv, in_sem,
+           hid, ids, slots, attn_norm, ffn_norm, moe_norm, w_router, cos_t, sin_t):
     me = lax.axis_index("ep")
     chip = me // 2
     core = me % 2
@@ -80,69 +83,47 @@
     mine = aligned(core, TOK)
     src_x, src_y, src_d = chip_x * 2 + core, chip_y * 2 + core, chip_d * 2 + core
 
+    def fetch(slot, src, part=None):
+        dst = ring.at[slot] if part is None else ring.at[(slot,) + part]
+        pltpu.make_async_copy(src, dst, ring_sem.at[slot]).start()
+
+    def fetch_ffn(slot, pair, mat):
+        fetch(slot, mat.at[:, aligned(core * FF_PAIRS + pair, CW)])
+
+    def fetch_expert(slot, expert, col, mat):
+        fetch(slot, mat.at[expert, :, aligned(col, CW)])
+
+    def fetch_down(slot, col, quad):
+        for i in range(4):
+            fetch(slot, exp_down.at[quad * 4 + i, :, aligned(col, BW)], (pl.ds(i // 2 * EFF, EFF), pl.ds(i % 2 * BW, BW)))
+
+    def fetch_ffn_down(slot, n, kk):
+        fetch(slot, ffn_down.at[aligned(core * N_FK + kk, DM), aligned(n, CW)])
+
     def start(g, slot):
-        def fetch(src, part=None):
-            dst = ring.at[slot] if part is None else ring.at[(slot,) + part]
-            pltpu.make_async_copy(src, dst, ring_sem.at[slot]).start()
-
         def within(lo, hi):
             return pl.when(jnp.logical_and(g >= lo, g < hi))
 
         @within(G_QKV, G_OUT)
         def _():
-            col, kind = g // 3, g % 3
             for which, mat in enumerate((w_query, w_key, w_value)):
-                @pl.when(kind == which)
-                def _():
-                    fetch(mat.at[:, aligned(col, CW)])
+                pl.when(g % 3 == which)(lambda mat=mat: fetch(slot, mat.at[:, aligned(g // 3, CW)]))
 
         @within(G_OUT, G_FFA)
         def _():
-            fetch(w_out.at[:, aligned(g - G_OUT, CW)])
-
-        def ff_pair(local, first):
-            col, kind = core * FF_PAIRS + first + local // 2, local % 2
-
-            @pl.when(kind == 0)
-            def _():
-                fetch(ffn_gate.at[:, aligned(col, CW)])
-
-            @pl.when(kind == 1)
-            def _():
-                fetch(ffn_up.at[:, aligned(col, CW)])
+            fetch(slot, w_out.at[:, aligned(g - G_OUT, CW)])
 
         @within(G_FFA, G_EGU)
         def _():
-            ff_pair(g - G_FFA, 0)
+            local = g - G_FFA
+            for which, mat in enumerate((ffn_gate, ffn_up)):
+                pl.when(local % 2 == which)(lambda mat=mat: fetch_ffn(slot, local // 2, mat))
 
         @within(G_EGU, G_EDN)
         def _():
             local = g - G_EGU
-            expert, col, kind = local // 4, (local // 2) % 2, local % 2
-
-            @pl.when(kind == 0)
-            def _():
-                fetch(exp_gate.at[expert, :, aligned(col, CW)])
-
-            @pl.when(kind == 1)
-            def _():
-                fetch(exp_up.at[expert, :, aligned(col, CW)])
-
-        @within(G_EDN, G_FFB)
-        def _():
-            local = g - G_EDN
-            col, quad = local // 2, local % 2
-            for i in range(4):
-                fetch(exp_down.at[quad * 4 + i, :, aligned(col, BW)], (pl.ds(i // 2 * EFF, EFF), pl.ds(i % 2 * BW, BW)))
-
-        @within(G_FFB, G_FDN)
-        def _():
-            ff_pair(g - G_FFB, FF_EARLY + FF_MID)
-
-        @within(G_FDN, G_END)
-        def _():
-            local = g - G_FDN
-            fetch(ffn_down.at[aligned(core * N_FK + local % N_FK, DM), aligned(local // N_FK, CW)])
+            for which, mat in enumerate((exp_gate, exp_up)):
+                pl.when(local % 2 == which)(lambda mat=mat: fetch_expert(slot, local // 4, local // 2 % 2, mat))
 
     def ready(g):
         slot = g % NSLOT
@@ -185,11 +166,23 @@
     def wait_got(block, sem):
         send(block, block, s2_send.at[0], sem, sib).wait_recv()
 
-    for g in range(NSLOT):
-        start(jnp.int32(g), g)
+    loads = {name: pltpu.make_async_copy(src, dst, in_sem.at[i]) for i, (name, src, dst) in enumerate((
+        ("hid", hid_h, hid), ("moe_norm", moe_norm_h, moe_norm), ("attn_norm", attn_norm_h, attn_norm),
+        ("w_router", w_router_h, w_router), ("ids", ids_h, ids), ("slots", slots_h, slots),
+        ("cos", cos_h, cos_t), ("sin", sin_h, sin_t), ("ffn_norm", ffn_norm_h, ffn_norm)))}
+
+    def loaded(*names):
+        for name in names:
+            loads[name].wait()
+
     barrier = pltpu.get_barrier_semaphore()
     for step in range(1, DEVS):
         pl.semaphore_signal(barrier, inc=1, device_id={"ep": (me + step) % DEVS}, device_id_type=pl.DeviceIdType.MESH)
+    for load in loads.values():
+        load.start()
+    loaded("hid", "moe_norm", "attn_norm", "w_router", "ids", "slots", "cos", "sin", "ffn_norm")
+    for g in range(NSLOT):
+        start(jnp.int32(g), g)
 
     hid_f = hid[...].astype(F32)
     inv_rms = lax.rsqrt(jnp.mean(hid_f * hid_f, axis=-1, keepdims=True) + RMS_EPS)
@@ -289,20 +282,27 @@
     x_block = xx.at[aligned(core, TOK)]
     x_copy = send(x_block, x_block, x_send, x_recv, sib)
 
-    def ffn_pair(g, col):
+    def ffn_pair(g, col, refill, between=None):
         slot = ready(g)
         slot_up = ready(g + 1)
+        if between is not None:
+            between()
         z_gate = dot(xx[...], ring[slot])
         z_up = dot(xx[...], ring[slot_up])
         hff[:, aligned(col, CW)] = silu_mul(z_gate, z_up)
-        done(g)
-        done(g + 1)
+        refill(slot, slot_up)
 
     def ffn_early(i, carry):
-        ffn_pair(G_FFA + 2 * i, i)
-        return carry
-
-    def dispatch(src, carry):
+        g = G_FFA + 2 * i
+
+        def refill(slot, slot_up):
+            done(g)
+            done(g + 1)
+
+        ffn_pair(g, i, refill)
+        return carry
+
+    def choose(src):
         want = lax.broadcasted_iota(jnp.int32, (ROWS, TOK), 0).astype(F32) + (me * ROWS).astype(F32)
         pick = jnp.zeros((ROWS, TOK), F32)
         gate = jnp.zeros((ROWS, TOK), F32)
@@ -318,11 +318,17 @@
         gates[src, 0:TOK, :] = high
         gates[src, TOK:2 * TOK, :] = mid
         gates[src, 2 * TOK:3 * TOK, :] = low
-        pick = pick.astype(BF16)
+        picks[...] = pick.astype(BF16)
+
+    def place(src):
         for cb in range(NCB):
-            rows = dot(pick, toks[src, cb * TOK:(cb + 1) * TOK, :]).astype(BF16)
+            rows = dot(picks[...], toks[src, cb * TOK:(cb + 1) * TOK, :]).astype(BF16)
             for e in range(LOCAL):
                 disp[e, pl.ds(pl.multiple_of(src * CAP, 16), CAP), cb * CW:(cb + 1) * CW] = rows[e * CAP:(e + 1) * CAP, :]
+
+    def dispatch(src, carry):
+        choose(src)
+        place(src)
         return carry
 
     def dispatch_two(one, two):
@@ -330,8 +336,8 @@
 
     wait_got(route.at[pl.ds(0, DEVS - 1)], rt_recv.at[0])
     ag_wait(4, 8)
+    x_copy.start()
     dispatch_two(me, sib)
-    x_copy.start()
     forward(src_x, (2, 3), 2, 9)
     forward(src_y, (0, 1), 5, 10)
     dispatch_two(src_x, src_y)
@@ -341,11 +347,14 @@
     ag_wait(4, 9)
     ag_wait(4, 10)
     forward(src_d, (0, 2), 6, 11)
-    dispatch_two(sib_x, sib_y)
+    dispatch(sib_x, 0)
     forward(src_d, (1, 3), 7, 11)
+    dispatch(sib_y, 0)
     lax.fori_loop(FF_EARLY, FF_EARLY + FF_MID, ffn_early, 0)
+    dispatch(src_d, 0)
+    choose(sib_d)
     ag_wait(4, 11)
-    dispatch_two(src_d, sib_d)
+    place(sib_d)
 
     wait_sent(toks.at[pl.ds(0, 7)], ag_send.at[0])
     wait_sent(route.at[pl.ds(0, DEVS - 1)], rt_send.at[0])
@@ -357,8 +366,16 @@
             z_gate = dot(disp[expert], ring[held[quarter * 2]])
             z_up = dot(disp[expert], ring[held[quarter * 2 + 1]])
             hexp[expert, :, quarter * 512:(quarter + 1) * 512] = silu_mul(z_gate, z_up)
-        for i in range(4):
-            done(g + i)
+
+        @pl.when(expert < LOCAL - 2)
+        def _():
+            for i in range(4):
+                fetch_expert(held[i], expert + 2, i // 2, (exp_gate, exp_up)[i % 2])
+
+        @pl.when(expert >= LOCAL - 2)
+        def _():
+            for i in range(4):
+                fetch_down(held[i], (expert - (LOCAL - 2)) * 2 + i // 2, i % 2)
         return carry
 
     lax.fori_loop(0, LOCAL, expert_up, 0)
@@ -387,15 +404,18 @@
             s2_copy(b, half).start()
 
     def down_block(b, carry):
-        def down_quad(quad):
-            g = G_EDN + b * 2 + quad
-            slot = ready(g)
+        def down_quad(quad, slot):
             for i in range(4):
                 e = quad * 4 + i
                 y = dot(hexp[e], ring[slot, i // 2 * EFF:(i // 2 + 1) * EFF, i % 2 * BW:(i % 2 + 1) * BW]).astype(BF16)
                 for s in range(DEVS):
                     toks[s, e * CAP:(e + 1) * CAP, 0:BW] = y[s * CAP:(s + 1) * CAP, :]
-            done(g)
+            pl.when(b < NBW - 4)(lambda: fetch_down(slot, b + 4, quad))
+            pl.when(b >= NBW - 4)(lambda: fetch_ffn(slot, FF_EARLY + FF_MID + b - (NBW - 4), (ffn_gate, ffn_up)[quad]))
+
+        def at(table, act):
+            for step, block in table:
+                pl.when(b == step)(functools.partial(act, block))
 
         def combine(dest, side):
             for name, c in (("d", chip_d), ("x", chip_x), ("y", chip_y), ("own", chip)):
@@ -404,43 +424,57 @@
                 for half in range(2):
                     dest[half, slot_of[name][half]] = moe[half * HALF:(half + 1) * HALF]
 
-        down_quad(0)
+        g = G_EDN + b * 2
+        slot = ready(g)
+        at(SEND2_START, send2)
+        down_quad(0, slot)
 
         @pl.when(b >= 1)
         def _():
             fold0(b - 1, False)
 
-        for step, block in FOLD1_AT:
-            pl.when(b == step)(functools.partial(fold1, block))
+        at(FOLD1_MID, fold1)
 
         @pl.when(b >= 2)
         def _():
             wait_sent(psib.at[b % 2], s0_send.at[b % 2])
 
-        down_quad(1)
-
-        @pl.when(b >= 1)
-        def _():
-            send1(b - 1)
-            fold0(b - 1, True)
-
-        for step, block in FOLD1_AT:
-            pl.when(b == step)(functools.partial(send2, block))
-
+        slot = ready(g + 1)
+        pl.when(b >= 1)(lambda: send1(b - 1))
+        at(FOLD1_MID, send2)
+        down_quad(1, slot)
+        pl.when(b >= 1)(lambda: fold0(b - 1, True))
         combine(psib.at[b % 2], 1 - core)
         start0(b, False)
         combine(pown.at[b], core)
         start0(b, True)
+        at(FOLD1_END, fold1)
         return carry
 
     lax.fori_loop(0, NBW, down_block, 0)
 
     def ffn_late(i, carry):
-        ffn_pair(G_FFB + 2 * i, FF_EARLY + FF_MID + i)
-
-        for step, act in (
-                (0, lambda: fold0(NBW - 1, False)), (1, lambda: send1(NBW - 1)), (1, lambda: fold1(4)),
-                (2, lambda: fold0(NBW - 1, True)), (2, lambda: send2(4)), (3, lambda: fold1(5)), (4, lambda: send2(5)), (5, lambda: fold1(6)), (6, lambda: send2(6))):
+        g = G_FFB + 2 * i
+
+        def refill(slot, slot_up):
+            pair = i + 4
+
+            @pl.when(pair < N_LATE)
+            def _():
+                fetch_ffn(slot, FF_EARLY + FF_MID + pair, ffn_gate)
+                fetch_ffn(slot_up, FF_EARLY + FF_MID + pair, ffn_up)
+
+            @pl.when(pair >= N_LATE)
+            def _():
+                fetch_ffn_down(slot, pair - N_LATE, 0)
+                fetch_ffn_down(slot_up, pair - N_LATE, 1)
+
+        def before():
+            for step, act in ((0, lambda: send2(4)), (1, lambda: send1(NBW - 1)), (2, lambda: send2(5)), (5, lambda: send2(6))):
+                pl.when(i == step)(act)
+
+        ffn_pair(g, FF_EARLY + FF_MID + i, refill, before)
+        for step, act in ((0, lambda: fold0(NBW - 1, False)), (1, lambda: fold0(NBW - 1, True)), (1, lambda: fold1(5)), (4, lambda: fold1(6))):
             pl.when(i == step)(act)
         return carry
 
@@ -450,15 +484,10 @@
         return send(fsend.at[n], frecv.at[n], f_send.at[0], f_recv.at[n], sib)
 
     def ffn_out(n, carry):
-        for kk in range(N_FK):
-            g = G_FDN + n * N_FK + kk
-            slot = ready(g)
-            part = dot(hff[:, kk * DM:(kk + 1) * DM], ring[slot])
-            done(g)
-            if kk == 0:
-                facc[...] = part
-            else:
-                facc[...] = facc[...] + part
+        g = G_FDN + n * N_FK
+        held = [ready(g + kk) for kk in range(N_FK)]
+        pl.when(n == 1)(lambda: send2(NBW - 1))
+        facc[...] = sum(dot(hff[:, kk * DM:(kk + 1) * DM], ring[held[kk]]) for kk in range(N_FK))
         fsend[n] = facc[aligned(1 - core, TOK), :]
         for w in range(CW // BW):
             b = n * (CW // BW) + w
@@ -466,8 +495,7 @@
                 own = facc[pl.ds(pl.multiple_of(core * TOK + half * HALF, HALF), HALF), w * BW:(w + 1) * BW]
                 pown[b, half, 0] = pown[b, half, 0] + own
         pl.when(n >= 1)(lambda: f_copy(n - 1).start())
-        for step, act in ((0, lambda: fold1(7)), (1, lambda: send2(7))):
-            pl.when(n == step)(act)
+        pl.when(n == 0)(lambda: fold1(NBW - 1))
         return carry
 
     lax.fori_loop(0, NCB, ffn_out, 0)
@@ -518,7 +546,7 @@
         call = pl.pallas_call(
             kernel,
             out_shape=pltpu.VMEM((TOK, DM), BF16),
-            in_specs=[vmem] * 9 + [hbm] * 10,
+            in_specs=[hbm] * 19,
             out_specs=vmem,
             scratch_shapes=[
                 pltpu.VMEM((NSLOT, DM, CW), BF16),
@@ -531,6 +559,7 @@
                 pltpu.VMEM((NBW, 2, 2, HALF, BW), F32),
                 pltpu.VMEM((NBW, 2, HALF, BW), F32),
                 pltpu.VMEM((DEVS, 3 * TOK, ROWS), BF16),
+                pltpu.VMEM((ROWS, TOK), BF16),
                 pltpu.VMEM((DEVS, 2 * TOPK, TOK), F32),
                 pltpu.VMEM((TOK, DM), BF16),
                 pltpu.VMEM((2 * TOK, DM), BF16),
@@ -544,7 +573,16 @@
                 pltpu.VMEM((TOK, CW), BF16),
                 dma((NSLOT,)), dma((1,)), dma((12,)), dma((1,)), dma((1,)),
                 dma((2,)), dma((NBW, 2)), dma((1,)), dma((NBW,)), dma((1,)), dma((NBW,)),
-                dma(()), dma(()), dma((1,)), dma((NCB,)),
+                dma(()), dma(()), dma((1,)), dma((NCB,)), dma((9,)),
+                pltpu.VMEM((TOK, DM), BF16),
+                pltpu.VMEM((TOPK, TOK), jnp.int32),
+                pltpu.VMEM((TOPK, TOK), jnp.int32),
+                pltpu.VMEM((DM // LANE, LANE), BF16),
+                pltpu.VMEM((DM // LANE, LANE), BF16),
+                pltpu.VMEM((DM // LANE, LANE), BF16),
+                pltpu.VMEM((NEXP, DM), BF16),
+                pltpu.VMEM((TOK, HEAD), F32),
+                pltpu.VMEM((TOK, HEAD), F32),
             ],
             compiler_params=pltpu.CompilerParams(collective_id=0, has_side_effects=True, vmem_limit_bytes=66000000),
             cost_estimate=pl.CostEstimate(flops=56_000_000_000, bytes_accessed=240_000_000, transcendentals=0),

time: 99.9 us -> 97 us (0.971)
  Pallas kernels: 99 us -> 96.1 us
    pallas_call x1, Pallas kernels: 99 us -> 96.1 us  [per_device(): call(hidden.reshape(TOK, DM), expert_ids.reshape(TOK, TOPK).T, slot_ids.r...]
where the time goes in v5:
time: 97 us; the launch traced here: 96.9 us
  Pallas kernels  96.1 us (99%)
    pallas_call x1, Pallas kernels, per_device(): call(hidden.reshape(TOK, DM), expert_ids.reshape(TOK, TOPK).T, slot_ids.r...  96.1 us

profile of v5, /device:TPU:0, one launch (start us, length us, event | category | flops | bytes accessed | tf_op | source)
XLA Modules:
  0.0 96.9 jit_solution(18098621425926536572)
XLA Ops:
  0.0 96.1 %shard_map.181 = bf16[128,2048]{1,0:T(8,128)(2,1)S(1)} custom-call(bf16[128,2048]{1,0:T(8,128)(2,1)} %bitcast.15, s32[8,128]{1,0:T(8,128)} %bitcast.17, s32[8,128]{1,0:T(8,128)} %bitcast.18, bf16[16,128]{1,0:T(8,128)(2,1)} %bitcast.19, bf16[16,128]{1,0:T(8,128)(2,1)} %bitcast.20, bf16[16,128]{1,0:T(8,128)(2,1)} %bitcast.21, bf16[64,2048]{1,0:T(8,128)(2,1)} %bitcast.16, ...), custom_call_target="tpu_custom_call" | custom-call | flops 56000000000 | bytes 240000000 | tf_op jit(solution)/shard_map/pallas_call | solution.py:590
  96.1 0.8 copy.21

commit v6 on v5

--- a/solution.py
+++ b/solution.py
@@ -35,7 +35,7 @@
 NBW = DM // BW
 FF_PAIRS = FF // 2 // CW
 NSLOT = 8
-FF_EARLY = 1
+FF_EARLY = 2
 FF_MID = 0
 
 N_QKV = 12
@@ -125,6 +125,17 @@
             for which, mat in enumerate((exp_gate, exp_up)):
                 pl.when(local % 2 == which)(lambda mat=mat: fetch_expert(slot, local // 4, local // 2 % 2, mat))
 
+    def start_now(g, slot):
+        if g < G_OUT:
+            fetch(slot, (w_query, w_key, w_value)[g % 3].at[:, pl.ds(g // 3 * CW, CW)])
+        elif g < G_FFA:
+            fetch(slot, w_out.at[:, pl.ds((g - G_OUT) * CW, CW)])
+        elif g < G_EGU:
+            fetch_ffn(slot, (g - G_FFA) // 2, (ffn_gate, ffn_up)[(g - G_FFA) % 2])
+        else:
+            local = g - G_EGU
+            fetch_expert(slot, local // 4, local // 2 % 2, (exp_gate, exp_up)[local % 2])
+
     def ready(g):
         slot = g % NSLOT
         pltpu.make_async_copy(w_query.at[:, pl.ds(0, CW)], ring.at[slot], ring_sem.at[slot]).wait()
@@ -182,7 +193,7 @@
         load.start()
     loaded("hid", "moe_norm", "attn_norm", "w_router", "ids", "slots", "cos", "sin", "ffn_norm")
     for g in range(NSLOT):
-        start(jnp.int32(g), g)
+        start_now(g, g)
 
     hid_f = hid[...].astype(F32)
     inv_rms = lax.rsqrt(jnp.mean(hid_f * hid_f, axis=-1, keepdims=True) + RMS_EPS)
@@ -191,13 +202,16 @@
         cb, within_cb = divmod(lt * LANE, CW)
         part = hid[:, cols].astype(F32) * inv_rms
         toks[me, cb * TOK:(cb + 1) * TOK, within_cb:within_cb + LANE] = (part * moe_norm[lt:lt + 1, :].astype(F32)).astype(BF16)
-        xx[mine, cols] = (part * attn_norm[lt:lt + 1, :].astype(F32)).astype(BF16)
 
     pl.semaphore_wait(barrier, DEVS - 1)
     for cb in range(NCB):
         ag_copy(me, cb, 0, min(cb, 2)).start()
         ag_copy(me, (cb + 2) % NCB, 1, 3 + min(cb, 2)).start()
         ag_copy(me, cb, 2, 8).start()
+
+    for lt in range(DM // LANE):
+        cols = slice(lt * LANE, (lt + 1) * LANE)
+        xx[mine, cols] = (hid[:, cols].astype(F32) * inv_rms * attn_norm[lt:lt + 1, :].astype(F32)).astype(BF16)
 
     logits = jnp.zeros((NEXP, TOK), F32)
     for cb in range(NCB):
@@ -229,51 +243,47 @@
             turned = part * cos_t[...] + pltpu.roll(part, HEAD // 2, 1) * sin_t[...]
             dst[:, h * HEAD:(h + 1) * HEAD] = turned.astype(BF16)
 
-    def attn_group(hg, carry):
-        g = G_QKV + hg * 3
-        slot = ready(g)
-        rope_into(qs, dot(xx[mine], ring[slot]))
-        done(g)
-
-        @pl.when(hg == 0)
-        def _():
-            for step in range(1, DEVS):
-                rt_copy(me, step).start()
-
-        slot = ready(g + 1)
-        rope_into(ks, dot(xx[mine], ring[slot]))
-        done(g + 1)
-        slot = ready(g + 2)
-        vs[...] = dot(xx[mine], ring[slot]).astype(BF16)
-        done(g + 2)
+    def heads(hg):
+        q, k, v = qs.at[hg % 2], ks.at[hg % 2], vs.at[hg % 2]
         for h in range(CW // HEAD):
             cols = slice(h * HEAD, (h + 1) * HEAD)
-            scores = lax.dot_general(qs[:, cols], ks[:, cols], (((1,), (1,)), ((), ())), preferred_element_type=F32) * HEAD ** -0.5
+            scores = lax.dot_general(q[:, cols], k[:, cols], (((1,), (1,)), ((), ())), preferred_element_type=F32) * HEAD ** -0.5
             scores = jnp.where(causal, scores, -jnp.inf)
             expd = jnp.exp(scores - jnp.max(scores, axis=-1, keepdims=True))
             prob = (expd / jnp.sum(expd, axis=-1, keepdims=True)).astype(BF16)
-            ctx[:, pl.ds(pl.multiple_of(hg * CW + h * HEAD, HEAD), HEAD)] = dot(prob, vs[:, cols]).astype(BF16)
-
-        @pl.when(hg == 2)
-        def _():
+            ctx[:, hg * CW + h * HEAD:hg * CW + (h + 1) * HEAD] = dot(prob, v[:, cols]).astype(BF16)
+
+    for hg in range(NCB):
+        g = G_QKV + hg * 3
+        held = [ready(g + i) for i in range(3)]
+        if hg:
+            heads(hg - 1)
+        rope_into(qs.at[hg % 2], dot(xx[mine], ring[held[0]]))
+        rope_into(ks.at[hg % 2], dot(xx[mine], ring[held[1]]))
+        vs[hg % 2] = dot(xx[mine], ring[held[2]]).astype(BF16)
+        for i in range(3):
+            start_now(g + i + NSLOT, held[i])
+        if hg == 0:
+            for step in range(1, DEVS):
+                rt_copy(me, step).start()
+        if hg == 2:
             relay(0, 0, 3, 6)
 
-        @pl.when(hg == 3)
-        def _():
-            relay(1, 1, 4, 7)
-        return carry
-
-    lax.fori_loop(0, NCB, attn_group, 0)
-
-    def out_block(n, carry):
-        g = G_OUT + n
-        slot = ready(g)
-        cols = aligned(n, CW)
-        a_s[:, cols] = (hid[:, cols].astype(F32) + dot(ctx[...], ring[slot])).astype(BF16)
-        done(g)
-        return carry
-
-    lax.fori_loop(0, N_OUT, out_block, 0)
+    def out_block(n, mixed):
+        cols = slice(n * CW, (n + 1) * CW)
+        a_s[:, cols] = (hid[:, cols].astype(F32) + mixed).astype(BF16)
+
+    slot = ready(G_OUT)
+    head_cols = (NCB - 1) * CW
+    mixed = dot(ctx[:, 0:head_cols], ring[slot, 0:head_cols, :])
+    heads(NCB - 1)
+    out_block(0, mixed + dot(ctx[:, head_cols:DM], ring[slot, head_cols:DM, :]))
+    start_now(G_OUT + NSLOT, slot)
+    relay(1, 1, 4, 7)
+    for n in range(1, N_OUT):
+        slot = ready(G_OUT + n)
+        out_block(n, dot(ctx[...], ring[slot]))
+        start_now(G_OUT + n + NSLOT, slot)
     a_f = a_s[...].astype(F32)
     inv_rms = lax.rsqrt(jnp.mean(a_f * a_f, axis=-1, keepdims=True) + RMS_EPS)
     for lt in range(DM // LANE):
@@ -486,7 +496,7 @@
     def ffn_out(n, carry):
         g = G_FDN + n * N_FK
         held = [ready(g + kk) for kk in range(N_FK)]
-        pl.when(n == 1)(lambda: send2(NBW - 1))
+        pl.when(n == 2)(lambda: send2(NBW - 1))
         facc[...] = sum(dot(hff[:, kk * DM:(kk + 1) * DM], ring[held[kk]]) for kk in range(N_FK))
         fsend[n] = facc[aligned(1 - core, TOK), :]
         for w in range(CW // BW):
@@ -495,7 +505,7 @@
                 own = facc[pl.ds(pl.multiple_of(core * TOK + half * HALF, HALF), HALF), w * BW:(w + 1) * BW]
                 pown[b, half, 0] = pown[b, half, 0] + own
         pl.when(n >= 1)(lambda: f_copy(n - 1).start())
-        pl.when(n == 0)(lambda: fold1(NBW - 1))
+        pl.when(n == 1)(lambda: fold1(NBW - 1))
         return carry
 
     lax.fori_loop(0, NCB, ffn_out, 0)
@@ -568,9 +578,9 @@
                 pltpu.VMEM((TOK, DM), BF16),
                 pltpu.VMEM((2 * TOK, FF // 2), BF16),
                 pltpu.VMEM((2 * TOK, CW), F32),
-                pltpu.VMEM((TOK, CW), BF16),
-                pltpu.VMEM((TOK, CW), BF16),
-                pltpu.VMEM((TOK, CW), BF16),
+                pltpu.VMEM((2, TOK, CW), BF16),
+                pltpu.VMEM((2, TOK, CW), BF16),
+                pltpu.VMEM((2, TOK, CW), BF16),
                 dma((NSLOT,)), dma((1,)), dma((12,)), dma((1,)), dma((1,)),
                 dma((2,)), dma((NBW, 2)), dma((1,)), dma((NBW,)), dma((1,)), dma((NBW,)),
                 dma(()), dma(()), dma((1,)), dma((NCB,)), dma((9,)),

time: 97 us -> 96.2 us (level)
  no operation moved by 1% of the time
where the time goes in v6:
time: 96.2 us; the launch traced here: 96.1 us
  Pallas kernels  95.3 us (99%)
    pallas_call x1, Pallas kernels, per_device(): call(hidden.reshape(TOK, DM), expert_ids.reshape(TOK, TOPK).T, slot_ids.r...  95.3 us

profile of v6, /device:TPU:0, one launch (start us, length us, event | category | flops | bytes accessed | tf_op | source)
XLA Modules:
  0.0 96.1 jit_solution(774924652011956471)
XLA Ops:
  0.0 95.3 %shard_map.181 = bf16[128,2048]{1,0:T(8,128)(2,1)S(1)} custom-call(bf16[128,2048]{1,0:T(8,128)(2,1)} %bitcast.15, s32[8,128]{1,0:T(8,128)} %bitcast.17, s32[8,128]{1,0:T(8,128)} %bitcast.18, bf16[16,128]{1,0:T(8,128)(2,1)} %bitcast.19, bf16[16,128]{1,0:T(8,128)(2,1)} %bitcast.20, bf16[16,128]{1,0:T(8,128)(2,1)} %bitcast.21, bf16[64,2048]{1,0:T(8,128)(2,1)} %bitcast.16, ...), custom_call_target="tpu_custom_call" | custom-call | flops 56000000000 | bytes 240000000 | tf_op jit(solution)/shard_map/pallas_call | solution.py:600
  95.3 0.8 copy.21

commit v7 on v6

--- a/solution.py
+++ b/solution.py
@@ -312,14 +312,21 @@
         ffn_pair(g, i, refill)
         return carry
 
+    def wanted_rows():
+        return lax.broadcasted_iota(jnp.int32, (ROWS, TOK), 0).astype(F32) + (me * ROWS).astype(F32)
+
     def choose(src):
-        want = lax.broadcasted_iota(jnp.int32, (ROWS, TOK), 0).astype(F32) + (me * ROWS).astype(F32)
+        want = wanted_rows()
         pick = jnp.zeros((ROWS, TOK), F32)
+        for j in range(TOPK):
+            pick = jnp.where(route[src, j:j + 1, :] == want, 1.0, pick)
+        picks[...] = pick.astype(BF16)
+
+    def weigh(src):
+        want = wanted_rows()
         gate = jnp.zeros((ROWS, TOK), F32)
         for j in range(TOPK):
-            hit = route[src, j:j + 1, :] == want
-            pick = jnp.where(hit, 1.0, pick)
-            gate = jnp.where(hit, route[src, TOPK + j:TOPK + j + 1, :], gate)
+            gate = jnp.where(route[src, j:j + 1, :] == want, route[src, TOPK + j:TOPK + j + 1, :], gate)
         gate_t = jnp.transpose(gate)
         high = gate_t.astype(BF16)
         rest = gate_t - high.astype(F32)
@@ -328,7 +335,6 @@
         gates[src, 0:TOK, :] = high
         gates[src, TOK:2 * TOK, :] = mid
         gates[src, 2 * TOK:3 * TOK, :] = low
-        picks[...] = pick.astype(BF16)
 
     def place(src):
         for cb in range(NCB):
@@ -372,6 +378,7 @@
     def expert_up(expert, carry):
         g = G_EGU + 4 * expert
         held = [ready(g + i) for i in range(4)]
+        weigh(expert)
         for quarter in range(2):
             z_gate = dot(disp[expert], ring[held[quarter * 2]])
             z_up = dot(disp[expert], ring[held[quarter * 2 + 1]])

time: 96.2 us -> 96.1 us (level)
  no operation moved by 1% of the time
where the time goes in v7:
time: 96.1 us; the launch traced here: 96 us
  Pallas kernels  95.2 us (99%)
    pallas_call x1, Pallas kernels, per_device(): call(hidden.reshape(TOK, DM), expert_ids.reshape(TOK, TOPK).T, slot_ids.r...  95.2 us

profile of v7, /device:TPU:0, one launch (start us, length us, event | category | flops | bytes accessed | tf_op | source)
XLA Modules:
  0.0 96.0 jit_solution(14179894638420713875)
XLA Ops:
  0.0 95.2 %shard_map.181 = bf16[128,2048]{1,0:T(8,128)(2,1)S(1)} custom-call(bf16[128,2048]{1,0:T(8,128)(2,1)} %bitcast.15, s32[8,128]{1,0:T(8,128)} %bitcast.17, s32[8,128]{1,0:T(8,128)} %bitcast.18, bf16[16,128]{1,0:T(8,128)(2,1)} %bitcast.19, bf16[16,128]{1,0:T(8,128)(2,1)} %bitcast.20, bf16[16,128]{1,0:T(8,128)(2,1)} %bitcast.21, bf16[64,2048]{1,0:T(8,128)(2,1)} %bitcast.16, ...), custom_call_target="tpu_custom_call" | custom-call | flops 56000000000 | bytes 240000000 | tf_op jit(solution)/shard_map/pallas_call | solution.py:607
  95.2 0.8 copy.21
